TPU v7x, 256 devices: a whole 4x4x8 slice. The times are simulated.
256 devices in a mesh: energy: 16 (over x, z_lo, core), kpt: 4 (over z_hi), layer: 4 (over y).
Axes of the slice: x: 4, y: 4, z: 8 (z_hi: 4, z_lo: 2; z = z_hi * 2 + z_lo), core: 2. Of those that a mesh axis runs over, the one named last changes fastest.
Arguments:
- energies: float32 [64], P(('energy', 'layer')), may hold values from -1.5 to 1.5
- momenta: float32 [4], P('kpt'), may hold values from 0 to 1
- energy_level: int32 [64], P(('energy', 'layer')), may hold values from 0 to 7
- momentum_level: int32 [4], P('kpt'), may hold values from 0 to 7
- energy_table: float32 [8], replicated, may hold values from 0.25 to 4
- momentum_table: float32 [8], replicated, may hold values from 0.25 to 4
- onsite: float32 [5, 256, 256], replicated, may hold values from -1 to 1, as said below
- broad: float32 [5, 256], replicated, may hold values from 1 to 4
- kdiag: float32 [5, 256], replicated, may hold values from 0.2 to 2
- fermi: float32 [5], replicated, may hold values from -1 to 1
- couplings: float32 [3, 256, 256], replicated, may hold values from -0.0624 to 0.0624
- bond_kind: int32 [4], replicated, may hold values from 0 to 2
Outputs:
- density: float32 [4, 2, 256, 256], P('layer', None, 'energy')
- current: float32 [4, 2, 256, 256], P('layer', None, 'energy')
Inputs may be any that keep to these rules, and one draw needn't show every extreme that they name: Each block of onsite is symmetric.
All inputs are finite; a program needn't handle non-finite values.
Results may differ from a plain program's by a relative error of at most 0.0001.
Values sent between devices are 32-bit elements; how exact they have to be, the bound alone decides.
No kernel may reach another device: no remote copies, remote signals or barrier semaphores. Data moves between devices by JAX's collectives and lax.ppermute only.
A program may use at most 64 MiB of HBM per device.

v0:
```python
import jax
import jax.numpy as jnp
from jax import lax
from jax.experimental import pallas as pl
from jax.experimental.pallas import tpu as pltpu
from jax.sharding import PartitionSpec as P

N = 256
ROWS = 256
CH = 32
f32 = jnp.float32
bf16 = jnp.bfloat16


def step_of(at, swap):
    first, second = at >> 1, at & 1
    plain = first ^ (3 * second)
    return plain ^ (swap * 2 * (first ^ second))


def slot_of(delta, swap):
    second = delta >> 1
    first = (delta & 1) ^ second
    plain = first * 2 + second
    return plain ^ (swap * 3 * (first ^ second))


def place():
    energy = lax.axis_index("energy")
    core = energy & 1
    return energy >> 2, lax.axis_index("layer"), (energy >> 1) & 1, core, core


def charge_kernel(pe, pk, elev, mlev, etab, mtab, fermi, kind, onsite, broad, kdiag, coup, keep, send, S, X, done):
    where_x, where_y, my_z, my_core, swap = place()
    slots = {}
    def slot(name):
        if name not in slots:
            slots[name] = len(slots)
            assert len(slots) <= S.shape[0], len(slots)
        return slots[name]
    fl = {}
    def fslot(name):
        if name not in fl:
            fl[name] = len(fl)
            assert len(fl) <= X.shape[0], len(fl)
        return fl[name]
    def put(name, r, x):
        i = slot(name)
        hi = x.astype(bf16)
        S[i, 0, r, :] = hi
        S[i, 1, r, :] = (x - hi.astype(f32)).astype(bf16)
    def mm(a, b, r, tb=False):
        a = slot(a); b = slot(b)
        dn = (((1,), (1 if tb else 0,)), ((), ()))
        d = lambda x, y: lax.dot_general(x, y, dn, preferred_element_type=f32)
        ah = S[a, 0, r, :]
        return d(ah, S[b, 0]) + d(ah, S[b, 1]) + d(S[a, 1, r, :], S[b, 0])
    def blocks(fn, post):
        for r0 in range(0, N, ROWS):
            vals = fn(slice(r0, r0 + ROWS))
            for c0 in range(0, ROWS, CH):
                post(slice(r0 + c0, r0 + c0 + CH), *[v[c0:c0 + CH] for v in vals])
    def pieces(post):
        for c0 in range(0, N, CH):
            post(slice(c0, c0 + CH))
    cols = lambda: lax.broadcasted_iota(jnp.int32, (CH, N), 1)
    def eye(r):
        return (lax.broadcasted_iota(jnp.int32, (CH, N), 0) + r.start) == cols()
    def result(comp, r, x):
        for c0 in range(0, r.stop - r.start, 16):
            done[comp, (r.start + c0) // 16] = x[c0:c0 + 16]
    def hand_out(layer):
        for core_at, to in ((0, keep), (1, send)):
            turn = swap ^ core_at
            y_at = slot_of(layer ^ where_y, turn)
            for x_at in range(4):
                x_from = where_x ^ step_of(x_at, turn)
                for z_at in range(2):
                    chunk = x_from * 4 + (my_z ^ z_at) * 2 + (my_core ^ core_at)
                    for comp in range(2):
                        to[0, x_at * 8 + y_at * 2 + z_at, comp] = done[comp, chunk]
                        to[1, y_at * 8 + x_at * 2 + z_at, comp] = done[2 + comp, chunk]
    e = pe[0]; k = pk[0]
    weight = etab[elev[0]] * mtab[mlev[0]] * (1.0 / 256)
    for i in range(4):
        def one(r, i=i):
            put(f"V{i}", r, coup[kind[i], r, :])
        pieces(one)
        vt = coup[kind[i]].T
        pieces(lambda r: put(f"Vt{i}", r, vt[r]))

    for i in range(5):
        shift = e - k * kdiag[i:i + 1, :]
        gamma = broad[i:i + 1, :] * jax.nn.sigmoid(jnp.full((1, N), (fermi[i] - e) / 0.25, f32))
        half = 0.5 * broad[i:i + 1, :]
        mr = fslot("mr"); mi = fslot("mi")
        if i:
            blocks(lambda r: (mm(f"Vt{i-1}", f"u{i-1}", r), mm(f"Vt{i-1}", f"v{i-1}", r)), lambda r, s, d: (
                X.__setitem__((mr, r), onsite[i, r, :] + 0.5 * (s + d)), X.__setitem__((mi, r), 0.5 * (s - d))))
            blocks(lambda r: (mm(f"Vt{i-1}", f"U{i-1}", r),), lambda r, y: put("C", r, y + jnp.where(eye(r), gamma, 0.0)))
            getr = lambda r: X[mr, r, :]
            geti = lambda r: X[mi, r, :]
        else:
            getr = lambda r: onsite[0, r, :]
        dr = jnp.zeros((1, N), f32); di = jnp.zeros((1, N), f32)
        for c0 in range(0, N, CH):
            r = slice(c0, c0 + CH)
            dr = dr + jnp.sum(jnp.where(eye(r), getr(r), 0.0), axis=0, keepdims=True)
            if i:
                di = di + jnp.sum(jnp.where(eye(r), geti(r), 0.0), axis=0, keepdims=True)
        dr = shift - dr
        di = half - di
        mod = dr * dr + di * di
        zr = dr / mod; zi = -di / mod
        size = jnp.sqrt(zr * zr + zi * zi)
        t = jnp.sqrt(0.5 * (size + jnp.abs(zr)))
        o = 0.5 * zi / t
        pos = zr >= 0.0
        rr = jnp.where(pos, t, jnp.abs(o))
        ri = jnp.where(pos, o, jnp.where(zi < 0.0, -t, t))
        crs = []; cis = []
        def outer(r):
            m = eye(r)
            cr = jnp.sum(jnp.where(m, rr, 0.0), axis=1, keepdims=True)
            ci = jnp.sum(jnp.where(m, ri, 0.0), axis=1, keepdims=True)
            return cr * rr - ci * ri, cr * ri + ci * rr
        orr = fslot("or"); oi = fslot("oi"); hr_ = fslot("hr"); hi_ = fslot("hi")
        def make_h(r):
            a, b = outer(r)
            X[orr, r] = a; X[oi, r] = b
            m = eye(r)
            er = jnp.where(m, 0.0, -getr(r))
            if i:
                ei = jnp.where(m, 0.0, -geti(r))
                hr = er * a - ei * b; hi = er * b + ei * a
            else:
                hr = er * a; hi = er * b
            X[hr_, r] = hr; X[hi_, r] = hi
            put("Hr", r, hr); put("Hi", r, hi); put("Hs", r, hr + hi)
        pieces(make_h)
        sr_ = fslot("sr"); si_ = fslot("si")
        def sq(r, a, b, c):
            sr = a - b
            X[sr_, r] = sr; X[si_, r] = c - a - b
            put("Sr", r, sr); put("Sa", r, c - 2.0 * a); put("Sb", r, c - 2.0 * b)
        blocks(lambda r: (mm("Hr", "Hr", r), mm("Hi", "Hi", r), mm("Hs", "Hs", r)), sq)
        def fin(r, k1, k2, k3):
            kr = X[sr_, r] - X[hr_, r] - (k1 - k3) + jnp.where(eye(r), 1.0, 0.0)
            ki = X[si_, r] - X[hi_, r] - (k1 + k2)
            a = X[orr, r]; b = X[oi, r]
            gr = kr * a - ki * b; gi = kr * b + ki * a
            gs = gr + gi; gd = gr - gi
            put(f"gs", r, gs); put(f"gd", r, gd)
            if 0 < i < 4:
                X[fslot(f"gs{i}"), r] = gs; X[fslot(f"gd{i}"), r] = gd
            if i == 4:
                put("Gs", r, gs); put("Gd", r, gd)
            if i == 0:
                put("p", r, gr * gamma); put("q", r, gi * gamma)
        blocks(lambda r: (mm("Hs", "Sr", r), mm("Hr", "Sa", r), mm("Hi", "Sb", r)), fin)
        if i < 4:
            blocks(lambda r: (mm("gs", f"V{i}", r), mm("gd", f"V{i}", r)), lambda r, u, v: (put(f"u{i}", r, u), put(f"v{i}", r, v)))
        if i:
            blocks(lambda r: (mm("gd", "C", r) + mm("gs", "C", r, True),), lambda r, p: put("p", r, 0.5 * p))
            blocks(lambda r: (mm("gs", "C", r), mm("gd", "C", r, True),), lambda r, a, b: put("q", r, 0.5 * (a - b)))
        w_ = fslot(f"w{i}")
        if i < 4:
            def keep_w(r, w):
                X[w_, r] = w
                put("W", r, w)
            blocks(lambda r: (mm("p", "gd", r) + mm("q", "gs", r),), keep_w)
            wt = X[w_].T
            pieces(lambda r: put("Wt", r, wt[r]))
            blocks(lambda r: (mm("W", f"V{i}", r), mm("Wt", f"V{i}", r)), lambda r, a, b: (put(f"U{i}", r, a), put(f"T{i}", r, b)))
        else:
            blocks(lambda r: (mm("p", "gd", r) + mm("q", "gs", r),), lambda r, w: put("W", r, w))

    for i in (3, 2, 1, 0):
        u = f"u{i}"; v = f"v{i}"; U = f"U{i}"; T = f"T{i}"
        def bond_r(r, a, b):
            result(2, r, (0.5 * weight) * (a + b))
            put("Yr", r, 0.25 * a + 0.5 * b)
        def bond_i(r, a, b, c, d):
            a = a - b; c = c - d
            result(3, r, (0.5 * weight) * (a + c))
            put("Yi", r, 0.25 * a + 0.5 * c)
        blocks(lambda r: (mm(v, "W", r) + mm(u, "W", r, True), mm(U, "Gs", r) + mm(T, "Gd", r)), bond_r)
        blocks(lambda r: (mm(u, "W", r), mm(v, "W", r, True), mm(U, "Gd", r), mm(T, "Gs", r)), bond_i)
        n_ = fslot("mr")
        def new_w(r, a, b):
            w = X[fslot(f"w{i}"), r] + a - b
            X[n_, r] = w
            if i:
                put("Wn", r, w)
        blocks(lambda r: (mm("Yr", v, r, True) + mm("Yi", u, r, True) + mm(u, "Yr", r, True), mm(v, "Yi", r, True)), new_w)
        wt = X[n_].T
        def dens(r):
            a = X[n_, r]; b = wt[r]
            result(0, r, (0.5 * weight) * (a + b))
            result(1, r, (0.5 * weight) * (a - b))
        pieces(dens)
        hand_out(i)
        slots["W"], slots["Wn"] = slots.get("Wn", 0), slots["W"]
        if i:
            blocks(lambda r: (mm(u, "Gd", r) + mm(v, "Gs", r),), lambda r, a: put("Qr", r, 0.5 * a))
            blocks(lambda r: (mm(u, "Gs", r), mm(v, "Gd", r)), lambda r, a, b: put("Qi", r, 0.5 * (a - b)))
            blocks(lambda r: (mm("Qr", u, r, True) + mm("Qi", v, r, True),), lambda r, a: put("Gs", r, X[fslot(f"gs{i}"), r] + a))
            blocks(lambda r: (mm("Qr", v, r, True), mm("Qi", u, r, True)), lambda r, a, b: put("Gd", r, X[fslot(f"gd{i}"), r] + a - b))


def charge(*arrays):
    smem = pl.BlockSpec(memory_space=pltpu.SMEM)
    vmem = pl.BlockSpec(memory_space=pltpu.VMEM)
    shape = jax.ShapeDtypeStruct((2, 32, 2, 16, N), f32)
    return pl.pallas_call(
        charge_kernel,
        out_shape=(shape, shape),
        in_specs=[smem] * 8 + [vmem] * 4,
        out_specs=(vmem, vmem),
        scratch_shapes=[
            pltpu.VMEM((48, 2, N, N), bf16),
            pltpu.VMEM((24, N, N), f32),
            pltpu.VMEM((4, 16, 16, N), f32),
        ],
        compiler_params=pltpu.CompilerParams(vmem_limit_bytes=56 * 1024 * 1024),
    )(*arrays)


def swapped(x, axes, partner):
    sizes = [lax.axis_size(a) for a in axes]
    count = 1
    for s in sizes:
        count *= s
    return lax.ppermute(x, axes, [(i, partner(i)) for i in range(count)])


def over_core(x):
    return swapped(x, ("energy",), lambda i: i ^ 1)


def over_x(x, turn):
    return swapped(x, ("energy",), lambda i: i ^ (12 if (i & 1) ^ turn else 4))


def over_y(x, turn):
    return swapped(x, ("energy", "layer"), lambda i: i ^ (3 if ((i >> 2) & 1) ^ turn else 1))


def over_z(x):
    return swapped(x, ("energy",), lambda i: i ^ 2)


def per_device(energies, momenta, energy_level, momentum_level, energy_table, momentum_table, onsite, broad, kdiag, fermi, couplings, bond_kind):
    keep, send = charge(energies, momenta, energy_level, momentum_level, energy_table, momentum_table, fermi, bond_kind, onsite, broad, kdiag, couplings)
    got = over_core(send)
    parts = [(keep[0], got[0]), (keep[1], got[1])]
    count = 32
    for across in ((over_x, over_y), (over_y, over_x)):
        for turn in range(2):
            count //= 2
            away = [mine[count:] + other[count:] for mine, other in parts]
            got = [across[g](away[g], turn) for g in range(2)]
            parts = [(mine[:count] + other[:count], got[g]) for g, (mine, other) in enumerate(parts)]
    away = jnp.stack([mine[1] + other[1] for mine, other in parts])
    got = over_z(away)
    mine = jnp.stack([mine[0] + other[0] for mine, other in parts]) + got
    near, far, last = (swapped(mine, ("kpt",), lambda i, s=s: i ^ s) for s in (1, 2, 3))
    total = (mine + near) + (far + last)
    return total[0][None], total[1][None]


def solution(mesh):
    return jax.shard_map(
        per_device,
        mesh=mesh,
        in_specs=(P(("energy", "layer")), P("kpt"), P(("energy", "layer")), P("kpt"), P(), P(), P(), P(), P(), P(), P(), P()),
        out_specs=(P("layer", None, "energy", None), P("layer", None, "energy", None)),
        check_vma=False,
    )
```

profile of v0, /device:TPU:38, one launch (start us, length us, event | category | flops | bytes accessed | tf_op | source)
XLA Modules:
  0.0 87.9 jit_solution(16237988774027462747)
XLA Ops:
  3.2 26.6 %shard_map.131 = (f32[2,32,2,16,256]{4,3,2,1,0:T(8,128)}, f32[2,32,2,16,256]{4,3,2,1,0:T(8,128)}) custom-call(f32[1]{0:T(128)S(6)} %copy.14.pe, f32[1]{0:T(128)S(6)} %copy.15.pk, s32[1]{0:T(128)S(6)} %copy.16.elev, s32[1]{0:T(128)S(6)} %copy.17.mlev, f32[8]{0:T(128)} %etab.1, f32[8]{0:T(128)} %mtab.1, f32[5]{0:T(128)} %fermi.1, s32[4]{0:T(128)} %kind.1, ...), custom_call_target="tpu_custom_call" | custom-call | tf_op jit(solution)/shard_map/pallas_call | solution.py:216
  29.8 0.0 collective-permute-start
  29.8 4.4 %collective-permute-done = f32[2,32,2,16,256]{4,3,2,1,0:T(8,128)S(1)} collective-permute-done((f32[2,32,2,16,256]{4,3,2,1,0:T(8,128)}, f32[2,32,2,16,256]{4,3,2,1,0:T(8,128)S(1)}, u32[]{:S(2)}, u32[]{:S(2)}) %collective-permute-start) | collective-permute-done | bytes 2097184 | tf_op jit(solution)/shard_map/ppermute | solution.py:235
  34.2 2.0 %slice_add_fusion.3 = (f32[1,16,2,16,256]{4,3,2,1,0:T(8,128)S(1)}, f32[16,2,16,256]{3,2,1,0:T(8,128)S(1)}, f32[1,16,2,16,256]{4,3,2,1,0:T(8,128)S(1)}, f32[16,2,16,256]{3,2,1,0:T(8,128)S(1)}) fusion(f32[2,32,2,16,256]{4,3,2,1,0:T(8,128)S(1)} %collective-permute-done, f32[2,32,2,16,256]{4,3,2,1,0:T(8,128)} %get-tuple-element.4), kind=kLoop, calls=%fused_computation.5 | loop fusion | flops 524288 | bytes 6291456 | tf_op jit(solution)/shard_map/add | solution.py:264
  36.2 1.7 %collective-permute-start.5 = (f32[16,2,16,256]{3,2,1,0:T(8,128)S(1)}, f32[16,2,16,256]{3,2,1,0:T(8,128)S(1)}, u32[]{:S(2)}, u32[]{:S(2)}) collective-permute-start(f32[16,2,16,256]{3,2,1,0:T(8,128)S(1)} %get-tuple-element.7), channel_id=1, source_target_pairs={{0,1},{1,0},{2,3},{3,2},{16,19},{17,18},{18,17},{19,16},{32,33},{3... | collective-permute-start | bytes 1572872 | tf_op jit(solution)/shard_map/ppermute | solution.py:235
  37.9 0.8 collective-permute-start.1
  38.7 6.8 %collective-permute-done.5 = f32[16,2,16,256]{3,2,1,0:T(8,128)S(1)} collective-permute-done((f32[16,2,16,256]{3,2,1,0:T(8,128)S(1)}, f32[16,2,16,256]{3,2,1,0:T(8,128)S(1)}, u32[]{:S(2)}, u32[]{:S(2)}) %collective-permute-start.5) | collective-permute-done | bytes 524320 | tf_op jit(solution)/shard_map/ppermute | solution.py:235
  45.5 0.1 slice_add_fusion.5
  45.6 3.1 %collective-permute-start.6 = (f32[8,2,16,256]{3,2,1,0:T(8,128)S(1)}, f32[8,2,16,256]{3,2,1,0:T(8,128)S(1)}, u32[]{:S(2)}, u32[]{:S(2)}) collective-permute-start(f32[8,2,16,256]{3,2,1,0:T(8,128)S(1)} %get-tuple-element.13), channel_id=1, source_target_pairs={{0,3},{1,2},{2,1},{3,0},{16,17},{17,16},{18,19},{19,18},{32,35},{3... | collective-permute-start | bytes 786440 | tf_op jit(solution)/shard_map/ppermute | solution.py:235
  48.7 0.0 collective-permute-done.1
  48.7 0.1 slice_add_fusion.7
  48.8 0.6 collective-permute-start.2
  49.3 3.9 %collective-permute-done.6 = f32[8,2,16,256]{3,2,1,0:T(8,128)S(1)} collective-permute-done((f32[8,2,16,256]{3,2,1,0:T(8,128)S(1)}, f32[8,2,16,256]{3,2,1,0:T(8,128)S(1)}, u32[]{:S(2)}, u32[]{:S(2)}) %collective-permute-start.6) | collective-permute-done | bytes 262176 | tf_op jit(solution)/shard_map/ppermute | solution.py:235
  53.3 0.9 %collective-permute-start.7 = (f32[4,2,16,256]{3,2,1,0:T(8,128)S(1)}, f32[4,2,16,256]{3,2,1,0:T(8,128)S(1)}, u32[]{:S(2)}, u32[]{:S(2)}) collective-permute-start(f32[4,2,16,256]{3,2,1,0:T(8,128)S(1)} %get-tuple-element.17), channel_id=1, source_target_pairs={{0,64},{16,208},{32,96},{48,240},{64,0},{80,144},{96,32},{112,176}... | collective-permute-start | bytes 393224 | tf_op jit(solution)/shard_map/ppermute | solution.py:235
  54.2 3.3 %collective-permute-done.2 = f32[8,2,16,256]{3,2,1,0:T(8,128)S(1)} collective-permute-done((f32[8,2,16,256]{3,2,1,0:T(8,128)S(1)}, f32[8,2,16,256]{3,2,1,0:T(8,128)S(1)}, u32[]{:S(2)}, u32[]{:S(2)}) %collective-permute-start.2) | collective-permute-done | bytes 262176 | tf_op jit(solution)/shard_map/ppermute | solution.py:235
  57.5 0.1 collective-permute-start.3
  57.6 0.7 collective-permute-done.7
  58.4 0.6 collective-permute-start.8
  58.9 4.3 %collective-permute-done.3 = f32[4,2,16,256]{3,2,1,0:T(8,128)S(1)} collective-permute-done((f32[4,2,16,256]{3,2,1,0:T(8,128)S(1)}, f32[4,2,16,256]{3,2,1,0:T(8,128)S(1)}, u32[]{:S(2)}, u32[]{:S(2)}) %collective-permute-start.3) | collective-permute-done | bytes 131104 | tf_op jit(solution)/shard_map/ppermute | solution.py:235
  63.2 0.1 collective-permute-start.4
  63.3 0.6 collective-permute-done.8
  63.9 4.8 %collective-permute-done.4 = f32[2,2,16,256]{3,2,1,0:T(8,128)S(1)} collective-permute-done((f32[2,2,16,256]{3,2,1,0:T(8,128)S(1)}, f32[2,2,16,256]{3,2,1,0:T(8,128)S(1)}, u32[]{:S(2)}, u32[]{:S(2)}) %collective-permute-start.4) | collective-permute-done | bytes 65568 | tf_op jit(solution)/shard_map/ppermute | solution.py:235
  68.8 0.2 collective-permute-start.9
  69.0 4.2 %collective-permute-done.9 = f32[2,2,16,256]{3,2,1,0:T(8,128)S(1)} collective-permute-done((f32[2,2,16,256]{3,2,1,0:T(8,128)S(1)}, f32[2,2,16,256]{3,2,1,0:T(8,128)S(1)}, u32[]{:S(2)}, u32[]{:S(2)}) %collective-permute-start.9) | collective-permute-done | bytes 65568 | tf_op jit(solution)/shard_map/ppermute | solution.py:235
  73.2 7.7 %collective-permute-start.11 = (f32[2,2,16,256]{3,2,1,0:T(8,128)S(1)}, f32[2,2,16,256]{3,2,1,0:T(8,128)S(1)}, u32[]{:S(2)}, u32[]{:S(2)}) collective-permute-start(f32[2,2,16,256]{3,2,1,0:T(8,128)S(1)} %maximum_add_fusion), channel_id=1, source_target_pairs={{0,8},{4,12},{8,0},{12,4},{1,9},{5,13},{9,1},{13,5},{2,10},{6,14},... | collective-permute-start | bytes 196616 | tf_op jit(solution)/shard_map/ppermute | solution.py:235
  80.9 0.0 collective-permute-start.12
  80.9 0.7 collective-permute-start.10
  81.6 2.5 %collective-permute-done.11 = f32[2,2,16,256]{3,2,1,0:T(8,128)S(1)} collective-permute-done((f32[2,2,16,256]{3,2,1,0:T(8,128)S(1)}, f32[2,2,16,256]{3,2,1,0:T(8,128)S(1)}, u32[]{:S(2)}, u32[]{:S(2)}) %collective-permute-start.11) | collective-permute-done | bytes 65568 | tf_op jit(solution)/shard_map/ppermute | solution.py:235
  84.1 3.2 %collective-permute-done.12 = f32[2,2,16,256]{3,2,1,0:T(8,128)S(1)} collective-permute-done((f32[2,2,16,256]{3,2,1,0:T(8,128)S(1)}, f32[2,2,16,256]{3,2,1,0:T(8,128)S(1)}, u32[]{:S(2)}, u32[]{:S(2)}) %collective-permute-start.12) | collective-permute-done | bytes 65568 | tf_op jit(solution)/shard_map/ppermute | solution.py:235
  87.3 0.0 collective-permute-done.10
  87.3 0.6 fusion.2
  (9 shorter events, 0.2 us)
Async XLA Ops:
  29.8 4.4 %collective-permute-start = (f32[2,32,2,16,256]{4,3,2,1,0:T(8,128)}, f32[2,32,2,16,256]{4,3,2,1,0:T(8,128)S(1)}, u32[]{:S(2)}, u32[]{:S(2)}) collective-permute-start(f32[2,32,2,16,256]{4,3,2,1,0:T(8,128)} %get-tuple-element.5), channel_id=1, source_target_pairs={{0,16},{16,0},{32,48},{48,32},{64,80},{80,64},{96,112},{112,96},{1... | collective-permute-start | bytes 6291464 | tf_op jit(solution)/shard_map/ppermute | solution.py:235
  36.2 9.3 %collective-permute-start.5 = (f32[16,2,16,256]{3,2,1,0:T(8,128)S(1)}, f32[16,2,16,256]{3,2,1,0:T(8,128)S(1)}, u32[]{:S(2)}, u32[]{:S(2)}) collective-permute-start(f32[16,2,16,256]{3,2,1,0:T(8,128)S(1)} %get-tuple-element.7), channel_id=1, source_target_pairs={{0,1},{1,0},{2,3},{3,2},{16,19},{17,18},{18,17},{19,16},{32,33},{3... | collective-permute-start | bytes 1572872 | tf_op jit(solution)/shard_map/ppermute | solution.py:235
  37.9 10.8 %collective-permute-start.1 = (f32[16,2,16,256]{3,2,1,0:T(8,128)S(1)}, f32[16,2,16,256]{3,2,1,0:T(8,128)S(1)}, u32[]{:S(2)}, u32[]{:S(2)}) collective-permute-start(f32[16,2,16,256]{3,2,1,0:T(8,128)S(1)} %get-tuple-element.9), channel_id=1, source_target_pairs={{0,64},{16,208},{32,96},{48,240},{64,0},{80,144},{96,32},{112,176}... | collective-permute-start | bytes 1572872 | tf_op jit(solution)/shard_map/ppermute | solution.py:235
  45.6 7.7 %collective-permute-start.6 = (f32[8,2,16,256]{3,2,1,0:T(8,128)S(1)}, f32[8,2,16,256]{3,2,1,0:T(8,128)S(1)}, u32[]{:S(2)}, u32[]{:S(2)}) collective-permute-start(f32[8,2,16,256]{3,2,1,0:T(8,128)S(1)} %get-tuple-element.13), channel_id=1, source_target_pairs={{0,3},{1,2},{2,1},{3,0},{16,17},{17,16},{18,19},{19,18},{32,35},{3... | collective-permute-start | bytes 786440 | tf_op jit(solution)/shard_map/ppermute | solution.py:235
  48.8 8.7 %collective-permute-start.2 = (f32[8,2,16,256]{3,2,1,0:T(8,128)S(1)}, f32[8,2,16,256]{3,2,1,0:T(8,128)S(1)}, u32[]{:S(2)}, u32[]{:S(2)}) collective-permute-start(f32[8,2,16,256]{3,2,1,0:T(8,128)S(1)} %get-tuple-element.11), channel_id=1, source_target_pairs={{0,192},{16,80},{32,224},{48,112},{64,128},{80,16},{96,160},{112,4... | collective-permute-start | bytes 786440 | tf_op jit(solution)/shard_map/ppermute | solution.py:235
  53.3 5.1 %collective-permute-start.7 = (f32[4,2,16,256]{3,2,1,0:T(8,128)S(1)}, f32[4,2,16,256]{3,2,1,0:T(8,128)S(1)}, u32[]{:S(2)}, u32[]{:S(2)}) collective-permute-start(f32[4,2,16,256]{3,2,1,0:T(8,128)S(1)} %get-tuple-element.17), channel_id=1, source_target_pairs={{0,64},{16,208},{32,96},{48,240},{64,0},{80,144},{96,32},{112,176}... | collective-permute-start | bytes 393224 | tf_op jit(solution)/shard_map/ppermute | solution.py:235
  57.5 5.7 %collective-permute-start.3 = (f32[4,2,16,256]{3,2,1,0:T(8,128)S(1)}, f32[4,2,16,256]{3,2,1,0:T(8,128)S(1)}, u32[]{:S(2)}, u32[]{:S(2)}) collective-permute-start(f32[4,2,16,256]{3,2,1,0:T(8,128)S(1)} %get-tuple-element.15), channel_id=1, source_target_pairs={{0,1},{1,0},{2,3},{3,2},{16,19},{17,18},{18,17},{19,16},{32,33},{3... | collective-permute-start | bytes 393224 | tf_op jit(solution)/shard_map/ppermute | solution.py:235
  58.4 5.6 %collective-permute-start.8 = (f32[2,2,16,256]{3,2,1,0:T(8,128)S(1)}, f32[2,2,16,256]{3,2,1,0:T(8,128)S(1)}, u32[]{:S(2)}, u32[]{:S(2)}) collective-permute-start(f32[2,2,16,256]{3,2,1,0:T(8,128)S(1)} %get-tuple-element.21), channel_id=1, source_target_pairs={{0,192},{16,80},{32,224},{48,112},{64,128},{80,16},{96,160},{112,4... | collective-permute-start | bytes 196616 | tf_op jit(solution)/shard_map/ppermute | solution.py:235
  63.2 5.6 %collective-permute-start.4 = (f32[2,2,16,256]{3,2,1,0:T(8,128)S(1)}, f32[2,2,16,256]{3,2,1,0:T(8,128)S(1)}, u32[]{:S(2)}, u32[]{:S(2)}) collective-permute-start(f32[2,2,16,256]{3,2,1,0:T(8,128)S(1)} %get-tuple-element.19), channel_id=1, source_target_pairs={{0,3},{1,2},{2,1},{3,0},{16,17},{17,16},{18,19},{19,18},{32,35},{3... | collective-permute-start | bytes 196616 | tf_op jit(solution)/shard_map/ppermute | solution.py:235
  68.8 4.4 %collective-permute-start.9 = (f32[2,2,16,256]{3,2,1,0:T(8,128)S(1)}, f32[2,2,16,256]{3,2,1,0:T(8,128)S(1)}, u32[]{:S(2)}, u32[]{:S(2)}) collective-permute-start(f32[2,2,16,256]{3,2,1,0:T(8,128)S(1)} %pad_maximum_fusion), channel_id=1, source_target_pairs={{0,32},{16,48},{32,0},{48,16},{64,96},{80,112},{96,64},{112,80},{1... | collective-permute-start | bytes 196616 | tf_op jit(solution)/shard_map/ppermute | solution.py:235
  73.2 10.9 %collective-permute-start.11 = (f32[2,2,16,256]{3,2,1,0:T(8,128)S(1)}, f32[2,2,16,256]{3,2,1,0:T(8,128)S(1)}, u32[]{:S(2)}, u32[]{:S(2)}) collective-permute-start(f32[2,2,16,256]{3,2,1,0:T(8,128)S(1)} %maximum_add_fusion), channel_id=1, source_target_pairs={{0,8},{4,12},{8,0},{12,4},{1,9},{5,13},{9,1},{13,5},{2,10},{6,14},... | collective-permute-start | bytes 196616 | tf_op jit(solution)/shard_map/ppermute | solution.py:235
  80.9 6.4 %collective-permute-start.12 = (f32[2,2,16,256]{3,2,1,0:T(8,128)S(1)}, f32[2,2,16,256]{3,2,1,0:T(8,128)S(1)}, u32[]{:S(2)}, u32[]{:S(2)}) collective-permute-start(f32[2,2,16,256]{3,2,1,0:T(8,128)S(1)} %maximum_add_fusion), channel_id=1, source_target_pairs={{0,12},{4,8},{8,4},{12,0},{1,13},{5,9},{9,5},{13,1},{2,14},{6,10},... | collective-permute-start | bytes 196616 | tf_op jit(solution)/shard_map/ppermute | solution.py:235
  80.9 6.4 %collective-permute-start.10 = (f32[2,2,16,256]{3,2,1,0:T(8,128)S(1)}, f32[2,2,16,256]{3,2,1,0:T(8,128)S(1)}, u32[]{:S(2)}, u32[]{:S(2)}) collective-permute-start(f32[2,2,16,256]{3,2,1,0:T(8,128)S(1)} %maximum_add_fusion), channel_id=1, source_target_pairs={{0,4},{4,0},{8,12},{12,8},{1,5},{5,1},{9,13},{13,9},{2,6},{6,2},{1... | collective-permute-start | bytes 196616 | tf_op jit(solution)/shard_map/ppermute | solution.py:235
where the time goes:
time: 88.1 us; the launch traced here: 87.9 us
  waiting for transfers between devices  38.7 us (44%)
  Pallas kernels  26.6 us (30%)
  starting transfers between devices  16.4 us (19%)
  between operations  3.3 us (4%)
  other arithmetic  2.35 us (3%)
    ppermute x13, waiting for transfers between devices, swapped(): return lax.ppermute(x, axes, [(i, partner(i)) for i in range(count)])  38.7 us
    pallas_call x1, Pallas kernels, charge(): pl.pallas_call(charge_kernel, out_shape=(shape, shape), in_specs=[smem] *...  26.6 us
    ppermute x13, starting transfers between devices, swapped(): return lax.ppermute(x, axes, [(i, partner(i)) for i in range(count)])  16.4 us
    add x7, other arithmetic, per_device(): mine[:count] + other[:count]  2.28 us
  transfers between devices with their start and end apart: 13, of which 11 were waited for; matrix products, arithmetic and copies ran while one was open for 0% of the time, Pallas kernels for 0%

commit v1 on v0

v1 whole, which is shorter than its diff:
```python
import jax
import jax.numpy as jnp
from jax import lax
from jax.experimental import pallas as pl
from jax.experimental.pallas import tpu as pltpu
from jax.sharding import PartitionSpec as P

N = 256
CH = 32
f32 = jnp.float32
bf16 = jnp.bfloat16
KEPT = ("u0", "v0", "U0", "T0", "u1", "v1", "U1", "T1", "W2", "Gs2", "Gd2", "Gs1", "Gd1")
KEPT_FULL = ("w0", "w1", "weight")


def step_of(at, swap):
    first, second = at >> 1, at & 1
    plain = first ^ (3 * second)
    return plain ^ (swap * 2 * (first ^ second))


class Parts:
    def __init__(self, pairs, full, kept_pairs=None, kept_full=None):
        self.pairs, self.full = pairs, full
        self.at, self.full_at = {}, {}
        self.kept = {} if kept_pairs is None else {n: (kept_pairs, i) for i, n in enumerate(KEPT)}
        self.kept_full = {} if kept_full is None else {n: (kept_full, i) for i, n in enumerate(KEPT_FULL)}

    def pair(self, name):
        if name in self.kept:
            return self.kept[name]
        i = self.at.setdefault(name, len(self.at))
        assert i < self.pairs.shape[0]
        return self.pairs, i

    def whole(self, name):
        if name in self.kept_full:
            return self.kept_full[name]
        i = self.full_at.setdefault(name, len(self.full_at))
        assert i < self.full.shape[0]
        return self.full, i

    def put(self, name, r, x):
        ref, i = self.pair(name)
        high = x.astype(bf16)
        ref[i, 0, r, :] = high
        ref[i, 1, r, :] = (x - high.astype(f32)).astype(bf16)

    def store(self, name, r, x):
        ref, i = self.whole(name)
        ref[i, r, :] = x

    def load(self, name, r):
        ref, i = self.whole(name)
        return ref[i, r, :]

    def turned(self, name):
        ref, i = self.whole(name)
        return ref[i].T

    def mm(self, left, right, turn=False):
        a, i = self.pair(left)
        b, j = self.pair(right)
        contract = (((1,), (1 if turn else 0,)), ((), ()))

        def dot(x, y):
            return lax.dot_general(x, y, contract, preferred_element_type=f32)

        high = a[i, 0]
        return dot(high, b[j, 0]) + dot(high, b[j, 1]) + dot(a[i, 1], b[j, 0])


def pieces(post, *values):
    for c0 in range(0, N, CH):
        r = slice(c0, c0 + CH)
        post(r, *[v[r] for v in values])


def eye(r):
    rows = lax.broadcasted_iota(jnp.int32, (CH, N), 0) + r.start
    return rows == lax.broadcasted_iota(jnp.int32, (CH, N), 1)


def hand_out(layer, done, keep, send):
    energy = lax.axis_index("energy")
    core = energy & 1
    my_x, my_z = energy >> 2, (energy >> 1) & 1
    where_y = lax.axis_index("layer")
    y_at = (layer ^ (layer >> 1) ^ where_y ^ (where_y >> 1)) & 1
    for core_at, to in ((0, keep), (1, send)):
        for x_at in range(4):
            x_from = my_x ^ step_of(x_at, core ^ core_at)
            for z_at in range(2):
                chunk = x_from * 4 + (my_z ^ z_at) * 2 + (core ^ core_at)
                for comp in range(4):
                    to[x_at * 4 + y_at * 2 + z_at, comp] = done[comp, chunk]


def back_products(m, i, weight, done):
    u, v, U, T = f"u{i}", f"v{i}", f"U{i}", f"T{i}"
    W, Gs, Gd = f"W{i + 1}", f"Gs{i + 1}", f"Gd{i + 1}"

    def result(comp, r, x):
        for c0 in range(0, CH, 16):
            done[comp, (r.start + c0) // 16] = x[c0 : c0 + 16]

    def bond_re(r, a, b):
        result(2, r, weight * (0.5 * (a + b)))
        m.put("Yr", r, 0.25 * a + 0.5 * b)

    def bond_im(r, a, b, c, d):
        a, c = a - b, c - d
        result(3, r, weight * (0.5 * (a + c)))
        m.put("Yi", r, 0.25 * a + 0.5 * c)

    def bond():
        pieces(bond_re, m.mm(v, W) + m.mm(u, W, True), m.mm(U, Gs) + m.mm(T, Gd))
        pieces(bond_im, m.mm(u, W), m.mm(v, W, True), m.mm(U, Gd), m.mm(T, Gs))

    def new_w(r, a, b):
        w = m.load(f"w{i}", r) + a - b
        m.store("Wfull", r, w)
        if i:
            m.put(f"W{i}", r, w)

    def density():
        pieces(new_w, m.mm("Yr", v, True) + m.mm("Yi", u, True) + m.mm(u, "Yr", True), m.mm(v, "Yi", True))

    def dens(r, turned):
        a = m.load("Wfull", r)
        result(0, r, weight * (0.5 * (a + turned)))
        result(1, r, weight * (0.5 * (a - turned)))

    def report():
        pieces(dens, m.turned("Wfull"))

    def carry():
        pieces(lambda r, a: m.put("Qr", r, 0.5 * a), m.mm(u, Gd) + m.mm(v, Gs))
        pieces(lambda r, a, b: m.put("Qi", r, 0.5 * (a - b)), m.mm(u, Gs), m.mm(v, Gd))

    def spread():
        pieces(lambda r, a: m.put(f"Gs{i}", r, m.load(f"gs{i}", r) + a), m.mm("Qr", u, True) + m.mm("Qi", v, True))
        pieces(lambda r, a, b: m.put(f"Gd{i}", r, m.load(f"gd{i}", r) + a - b), m.mm("Qr", v, True), m.mm("Qi", u, True))

    return bond, density, report, carry, spread


def forward_kernel(*refs):
    arrays, (keep, send, kept_pairs, kept_full, pairs, full, done), local, sems = refs[4:12], refs[12:19], refs[19:27], refs[27]
    pe, pk, elev, mlev = refs[:4]
    etab, mtab, fermi, kind, broad, kdiag, onsite, coup = local
    small = [pltpu.make_async_copy(arrays[n], local[n], sems.at[n]) for n in range(6)]
    blocks = [pltpu.make_async_copy(arrays[6].at[n], onsite.at[n], sems.at[6 + n]) for n in range(5)]
    hops = pltpu.make_async_copy(arrays[7], coup, sems.at[11])
    for copy in small + blocks[:1] + [hops] + blocks[1:]:
        copy.start()
    m = Parts(pairs, full, kept_pairs, kept_full)
    for copy in small:
        copy.wait()
    e = pe[0]
    k = pk[0]
    weight = jnp.full((1, N), etab[elev[0]] * mtab[mlev[0]] * (1.0 / 256), f32)
    kept_full[KEPT_FULL.index("weight"), 0:8, :] = jnp.broadcast_to(weight, (8, N))

    def source(i):
        return broad[i : i + 1, :] * jax.nn.sigmoid(jnp.full((1, N), (fermi[i] - e) / 0.25, f32))

    def real_part(i, r):
        return m.load("mr", r) if i else onsite[0, r, :]

    def own_energy(i):
        def post(r, s, d):
            m.store("mr", r, onsite[i, r, :] + 0.5 * (s + d))
            m.store("mi", r, 0.5 * (s - d))

        blocks[i].wait()
        pieces(post, m.mm(f"Vt{i - 1}", f"u{i - 1}"), m.mm(f"Vt{i - 1}", f"v{i - 1}"))

    def scale(i):
        dr = jnp.zeros((1, N), f32)
        di = jnp.zeros((1, N), f32)
        for c0 in range(0, N, CH):
            r = slice(c0, c0 + CH)
            dr = dr + jnp.sum(jnp.where(eye(r), real_part(i, r), 0.0), axis=0, keepdims=True)
            if i:
                di = di + jnp.sum(jnp.where(eye(r), m.load("mi", r), 0.0), axis=0, keepdims=True)
        dr = e - k * kdiag[i : i + 1, :] - dr
        di = 0.5 * broad[i : i + 1, :] - di
        modulus = dr * dr + di * di
        zr = dr / modulus
        zi = -di / modulus
        size = jnp.sqrt(zr * zr + zi * zi)
        large = jnp.sqrt(0.5 * (size + jnp.abs(zr)))
        other = 0.5 * zi / large
        rr = jnp.where(zr >= 0.0, large, jnp.abs(other))
        ri = jnp.where(zr >= 0.0, other, jnp.where(zi < 0.0, -large, large))

        def post(r):
            mask = eye(r)
            cr = jnp.sum(jnp.where(mask, rr, 0.0), axis=1, keepdims=True)
            ci = jnp.sum(jnp.where(mask, ri, 0.0), axis=1, keepdims=True)
            a = cr * rr - ci * ri
            b = cr * ri + ci * rr
            m.store("or", r, a)
            m.store("oi", r, b)
            er = jnp.where(mask, 0.0, -real_part(i, r))
            if i:
                ei = jnp.where(mask, 0.0, -m.load("mi", r))
                hr, hi = er * a - ei * b, er * b + ei * a
            else:
                hr, hi = er * a, er * b
            m.store("hr", r, hr)
            m.store("hi", r, hi)
            m.put("Hr", r, hr)
            m.put("Hi", r, hi)
            m.put("Hs", r, hr + hi)

        pieces(post)

    def square(i):
        def post(r, a, b, c):
            m.store("sr", r, a - b)
            m.store("si", r, c - a - b)
            m.put("Sr", r, a - b)
            m.put("Sa", r, c - 2.0 * a)
            m.put("Sb", r, c - 2.0 * b)

        pieces(post, m.mm("Hr", "Hr"), m.mm("Hi", "Hi"), m.mm("Hs", "Hs"))

    def green(i):
        def post(r, k1, k2, k3):
            kr = m.load("sr", r) - m.load("hr", r) - (k1 - k3) + jnp.where(eye(r), 1.0, 0.0)
            ki = m.load("si", r) - m.load("hi", r) - (k1 + k2)
            a = m.load("or", r)
            b = m.load("oi", r)
            gr = kr * a - ki * b
            gi = kr * b + ki * a
            m.put(f"Gs{i}" if i == 4 else f"s{i % 2}", r, gr + gi)
            m.put(f"Gd{i}" if i == 4 else f"d{i % 2}", r, gr - gi)
            if 0 < i < 4:
                m.store(f"gs{i}", r, gr + gi)
                m.store(f"gd{i}", r, gr - gi)
            if i == 0:
                m.put("p0", r, gr * source(0))
                m.put("q0", r, gi * source(0))

        pieces(post, m.mm("Hs", "Sr"), m.mm("Hr", "Sa"), m.mm("Hi", "Sb"))

    def hop(i):
        pieces(lambda r, u, v: (m.put(f"u{i}", r, u), m.put(f"v{i}", r, v)), m.mm(f"s{i % 2}", f"V{i}"), m.mm(f"d{i % 2}", f"V{i}"))

    def names(i):
        return ("Gs4", "Gd4") if i == 4 else (f"s{i % 2}", f"d{i % 2}")

    def inflow(i):
        gamma = source(i)
        pieces(lambda r, y: m.put(f"C{i % 2}", r, y + jnp.where(eye(r), gamma, 0.0)), m.mm(f"Vt{i - 1}", f"U{i - 1}"))

    def dressed(i):
        s, d = names(i)
        C = f"C{i % 2}"
        pieces(lambda r, p: m.put(f"p{i % 2}", r, 0.5 * p), m.mm(d, C) + m.mm(s, C, True))
        pieces(lambda r, a, b: m.put(f"q{i % 2}", r, 0.5 * (a - b)), m.mm(s, C), m.mm(d, C, True))

    def lesser(i):
        s, d = names(i)

        def post(r, w):
            if i < 4:
                m.store(f"w{i}", r, w)
                m.put("Wl", r, w)
            else:
                m.put("W4", r, w)

        pieces(post, m.mm(f"p{i % 2}", d) + m.mm(f"q{i % 2}", s))

    def lesser_turned(i):
        pieces(lambda r, x: m.put("Wt", r, x), m.turned(f"w{i}"))

    def lesser_hop(i):
        pieces(lambda r, a, b: (m.put(f"U{i}", r, a), m.put(f"T{i}", r, b)), m.mm("Wl", f"V{i}"), m.mm("Wt", f"V{i}"))

    blocks[0].wait()
    scale(0)
    square(0)
    hops.wait()
    for i in range(4):
        pieces(lambda r, x: m.put(f"V{i}", r, x), coup[kind[i]])
        pieces(lambda r, x: m.put(f"Vt{i}", r, x), coup[kind[i]].T)
    green(0)
    hop(0)
    for i in range(1, 5):
        own_energy(i)
        if i > 1:
            dressed(i - 1)
        scale(i)
        lesser(i - 1)
        square(i)
        lesser_turned(i - 1)
        green(i)
        lesser_hop(i - 1)
        if i < 4:
            hop(i)
        inflow(i)
    steps = {i: back_products(m, i, weight, done) for i in (3, 2, 1)}
    dressed(4)
    steps[3][3]()
    lesser(4)
    steps[3][4]()
    steps[3][0]()
    steps[2][3]()
    steps[3][1]()
    steps[2][4]()
    steps[3][2]()
    hand_out(3, done, keep, send)
    steps[2][0]()
    steps[1][3]()
    steps[2][1]()
    steps[1][4]()
    steps[2][2]()
    hand_out(2, done, keep, send)


def backward_kernel(kept_pairs, kept_full, keep, send, pairs, full, done):
    m = Parts(pairs, full, kept_pairs, kept_full)
    weight = kept_full[KEPT_FULL.index("weight"), 0:1, :]
    for i in (1, 0):
        bond, density, report, _, _ = back_products(m, i, weight, done)
        bond()
        density()
        report()
        hand_out(i, done, keep, send)


def cost(products):
    return pl.CostEstimate(flops=products * 6 * N**3, bytes_accessed=8 * 2**20, transcendentals=0)


BLOCK = (16, 4, 16, N)


def forward(arrays):
    smem = pl.BlockSpec(memory_space=pltpu.SMEM)
    vmem = pl.BlockSpec(memory_space=pltpu.VMEM)
    hbm = pl.BlockSpec(memory_space=pltpu.HBM)
    return pl.pallas_call(
        forward_kernel,
        out_shape=(
            jax.ShapeDtypeStruct(BLOCK, f32),
            jax.ShapeDtypeStruct(BLOCK, f32),
            jax.ShapeDtypeStruct((len(KEPT), 2, N, N), bf16),
            jax.ShapeDtypeStruct((len(KEPT_FULL), N, N), f32),
        ),
        in_specs=[smem] * 4 + [hbm] * 8,
        out_specs=(vmem,) * 4,
        scratch_shapes=[
            pltpu.VMEM((56, 2, N, N), bf16),
            pltpu.VMEM((18, N, N), f32),
            pltpu.VMEM((4, 16, 16, N), f32),
            pltpu.SMEM((8,), f32),
            pltpu.SMEM((8,), f32),
            pltpu.SMEM((5,), f32),
            pltpu.SMEM((4,), jnp.int32),
            pltpu.VMEM((5, N), f32),
            pltpu.VMEM((5, N), f32),
            pltpu.VMEM((5, N, N), f32),
            pltpu.VMEM((3, N, N), f32),
            pltpu.SemaphoreType.DMA((12,)),
        ],
        compiler_params=pltpu.CompilerParams(vmem_limit_bytes=44 * 1024 * 1024),
        cost_estimate=cost(132),
    )(*arrays[:4], *[pltpu.with_memory_space_constraint(a, pltpu.HBM) for a in arrays[4:]])


def backward(kept_pairs, kept_full):
    vmem = pl.BlockSpec(memory_space=pltpu.VMEM)
    return pl.pallas_call(
        backward_kernel,
        out_shape=(jax.ShapeDtypeStruct(BLOCK, f32), jax.ShapeDtypeStruct(BLOCK, f32)),
        in_specs=[vmem] * 2,
        out_specs=(vmem,) * 2,
        scratch_shapes=[
            pltpu.VMEM((4, 2, N, N), bf16),
            pltpu.VMEM((2, N, N), f32),
            pltpu.VMEM((4, 16, 16, N), f32),
        ],
        compiler_params=pltpu.CompilerParams(vmem_limit_bytes=12 * 1024 * 1024),
        cost_estimate=cost(24),
    )(kept_pairs, kept_full)


def swapped(x, axes, partner):
    count = 1
    for a in axes:
        count *= lax.axis_size(a)
    return lax.ppermute(x, axes, [(i, partner(i)) for i in range(count)])


def over_core(x):
    return swapped(x, ("energy",), lambda i: i ^ 1)


def over_x(x, turn):
    return swapped(x, ("energy",), lambda i: i ^ (12 if (i & 1) ^ turn else 4))


def over_y(x, step):
    return swapped(x, ("layer",), lambda i: i ^ step)


def over_z(x):
    return swapped(x, ("energy",), lambda i: i ^ 2)


def to_one_block(keep, got):
    mine, other = keep, got
    count = 16
    for across in (lambda x: over_x(x, 0), lambda x: over_x(x, 1), lambda x: over_y(x, 1), over_z):
        count //= 2
        away = mine[count:] + other[count:]
        mine, other = mine[:count] + other[:count], across(away)
    return mine[0] + other[0]


def per_device(energies, momenta, energy_level, momentum_level, energy_table, momentum_table, onsite, broad, kdiag, fermi, couplings, bond_kind):
    keep_high, send_high, kept_pairs, kept_full = forward(
        (energies, momenta, energy_level, momentum_level, energy_table, momentum_table, fermi, bond_kind, broad, kdiag, onsite, couplings)
    )
    got_high = over_core(send_high)
    keep_low, send_low = backward(kept_pairs, kept_full)
    got_low = over_core(send_low)
    high = to_one_block(keep_high, got_high)
    low = to_one_block(keep_low, got_low)
    upper = lax.axis_index("layer") >= 2
    got = over_y(jnp.where(upper, low, high), 3)
    mine = jnp.where(upper, high, low) + got
    near, far, last = (swapped(mine, ("kpt",), lambda i, s=s: i ^ s) for s in (1, 2, 3))
    total = (mine + near) + (far + last)
    return total[None, :2], total[None, 2:]


def solution(mesh):
    return jax.shard_map(
        per_device,
        mesh=mesh,
        in_specs=(P(("energy", "layer")), P("kpt"), P(("energy", "layer")), P("kpt"), P(), P(), P(), P(), P(), P(), P(), P()),
        out_specs=(P("layer", None, "energy", None), P("layer", None, "energy", None)),
        check_vma=False,
    )
```

time: 88.1 us -> 82.7 us (0.939); the launches traced: 87.9 us -> 81.4 us
  Pallas kernels: 26.6 us -> 22.5 us
  waiting for transfers between devices: 38.7 us -> 35.9 us
  starting transfers between devices: 16.4 us -> 18.3 us
  other arithmetic: 2.35 us -> 0.81 us
    pallas_call x1 -> x2, Pallas kernels: 26.6 us -> 22.5 us  [the longest x1 19 us: forward(): pl.pallas_call(forward_kernel, out_shape=(jax.ShapeDtypeStruct(BLOCK, f32...]
    ppermute x13 -> x14, waiting for transfers between devices: 38.7 us -> 35.9 us  [swapped(): return lax.ppermute(x, axes, [(i, partner(i)) for i in range(count)])]
    ppermute x13 -> x14, starting transfers between devices: 16.4 us -> 18.3 us  [swapped(): return lax.ppermute(x, axes, [(i, partner(i)) for i in range(count)])]
    add x10 -> x9, other arithmetic: 2.31 us -> 0.76 us  [the longest x6 0.71 us: to_one_block(): mine, other = (mine[:count] + other[:count], across(away))]
  transfers between devices with their start and end apart: 13 -> 14, of which waited for: 11 -> 10; matrix products, arithmetic and copies ran while one was open for 0% -> 1% of each run, Pallas kernels for 0% -> 4%
where the time goes in v1:
time: 82.7 us; the launch traced here: 81.4 us
  waiting for transfers between devices  35.9 us (43%)
  Pallas kernels  22.5 us (27%)
  starting transfers between devices  18.3 us (22%)
  between operations  3.3 us (4%)
    ppermute x14, waiting for transfers between devices, swapped(): return lax.ppermute(x, axes, [(i, partner(i)) for i in range(count)])  35.9 us
    pallas_call x1, Pallas kernels, forward(): pl.pallas_call(forward_kernel, out_shape=(jax.ShapeDtypeStruct(BLOCK, f32...  19 us
    ppermute x14, starting transfers between devices, swapped(): return lax.ppermute(x, axes, [(i, partner(i)) for i in range(count)])  18.3 us
    pallas_call x1, Pallas kernels, backward(): pl.pallas_call(backward_kernel, out_shape=(jax.ShapeDtypeStruct(BLOCK, f3...  3.48 us
  transfers between devices with their start and end apart: 14, of which 10 were waited for; matrix products, arithmetic and copies ran while one was open for 1% of the time, Pallas kernels for 4%

profile of v1, /device:TPU:38, one launch (start us, length us, event | category | flops | bytes accessed | tf_op | source)
XLA Modules:
  0.0 81.4 jit_solution(10991768149365865976)
XLA Ops:
  3.2 19.0 %shard_map.131 = (f32[16,4,16,256]{3,2,1,0:T(8,128)S(1)}, f32[16,4,16,256]{3,2,1,0:T(8,128)S(1)}, bf16[13,2,256,256]{3,2,1,0:T(8,128)(2,1)S(1)}, f32[3,256,256]{2,1,0:T(8,128)S(1)}) custom-call(f32[1]{0:T(128)S(6)} %copy.14.refs_0_, f32[1]{0:T(128)S(6)} %copy.15.refs_1_, s32[1]{0:T(128)S(6)} %copy.16.refs_2_, s32[1]{0:T(128)S(6)} %copy.17.refs_3_, ...), custom_call_target="tpu_custom_call" | custom-call | flops 13287555072 | bytes 8388608 | tf_op jit(solution)/shard_map/pallas_call | solution.py:346
  22.2 0.1 collective-permute-start
  22.3 3.5 %shard_map.132 = (f32[16,4,16,256]{3,2,1,0:T(8,128)S(1)}, f32[16,4,16,256]{3,2,1,0:T(8,128)S(1)}) custom-call(bf16[13,2,256,256]{3,2,1,0:T(8,128)(2,1)S(1)} %get-tuple-element.10.kept_pairs, f32[3,256,256]{2,1,0:T(8,128)S(1)} %get-tuple-element.11.kept_full), custom_call_target="tpu_custom_call" | custom-call | flops 2415919104 | bytes 8388608 | tf_op jit(solution)/shard_map/pallas_call | solution.py:377
  25.8 0.6 collective-permute-start.5
  26.4 0.0 collective-permute-done
  26.4 0.2 slice_add_fusion.3
  26.6 0.9 %collective-permute-start.1 = (f32[8,4,16,256]{3,2,1,0:T(8,128)S(1)}, f32[8,4,16,256]{3,2,1,0:T(8,128)S(1)}, u32[]{:S(2)}, u32[]{:S(2)}) collective-permute-start(f32[8,4,16,256]{3,2,1,0:T(8,128)S(1)} %get-tuple-element.17), channel_id=1, source_target_pairs={{0,64},{16,208},{32,96},{48,240},{64,0},{80,144},{96,32},{112,176}... | collective-permute-start | bytes 1572872 | tf_op jit(solution)/shard_map/ppermute | solution.py:396
  27.5 1.1 %collective-permute-done.5 = f32[16,4,16,256]{3,2,1,0:T(8,128)S(1)} collective-permute-done((f32[16,4,16,256]{3,2,1,0:T(8,128)S(1)}, f32[16,4,16,256]{3,2,1,0:T(8,128)S(1)}, u32[]{:S(2)}, u32[]{:S(2)}) %collective-permute-start.5) | collective-permute-done | bytes 1048608 | tf_op jit(solution)/shard_map/ppermute | solution.py:396
  28.7 0.2 slice_add_fusion.1
  28.9 0.9 %collective-permute-start.6 = (f32[8,4,16,256]{3,2,1,0:T(8,128)S(1)}, f32[8,4,16,256]{3,2,1,0:T(8,128)S(1)}, u32[]{:S(2)}, u32[]{:S(2)}) collective-permute-start(f32[8,4,16,256]{3,2,1,0:T(8,128)S(1)} %get-tuple-element.15), channel_id=1, source_target_pairs={{0,64},{16,208},{32,96},{48,240},{64,0},{80,144},{96,32},{112,176}... | collective-permute-start | bytes 1572872 | tf_op jit(solution)/shard_map/ppermute | solution.py:396
  29.8 6.1 %collective-permute-done.1 = f32[8,4,16,256]{3,2,1,0:T(8,128)S(1)} collective-permute-done((f32[8,4,16,256]{3,2,1,0:T(8,128)S(1)}, f32[8,4,16,256]{3,2,1,0:T(8,128)S(1)}, u32[]{:S(2)}, u32[]{:S(2)}) %collective-permute-start.1) | collective-permute-done | bytes 524320 | tf_op jit(solution)/shard_map/ppermute | solution.py:396
  35.9 0.1 slice_add_fusion.7
  36.0 0.6 collective-permute-start.2
  36.5 7.7 %collective-permute-done.6 = f32[8,4,16,256]{3,2,1,0:T(8,128)S(1)} collective-permute-done((f32[8,4,16,256]{3,2,1,0:T(8,128)S(1)}, f32[8,4,16,256]{3,2,1,0:T(8,128)S(1)}, u32[]{:S(2)}, u32[]{:S(2)}) %collective-permute-start.6) | collective-permute-done | bytes 524320 | tf_op jit(solution)/shard_map/ppermute | solution.py:396
  44.3 0.1 slice_add_fusion.5
  44.4 0.6 collective-permute-start.7
  44.9 0.0 collective-permute-done.2
  45.0 1.7 %collective-permute-start.3 = (f32[2,4,16,256]{3,2,1,0:T(8,128)S(1)}, f32[2,4,16,256]{3,2,1,0:T(8,128)S(1)}, u32[]{:S(2)}, u32[]{:S(2)}) collective-permute-start(f32[2,4,16,256]{3,2,1,0:T(8,128)S(1)} %get-tuple-element.25), channel_id=1, source_target_pairs={{0,1},{1,0},{2,3},{3,2},{4,5},{5,4},{6,7},{7,6},{8,9},{9,8},{10,11... | collective-permute-start | bytes 393224 | tf_op jit(solution)/shard_map/ppermute | solution.py:396
  46.6 5.4 %collective-permute-done.7 = f32[4,4,16,256]{3,2,1,0:T(8,128)S(1)} collective-permute-done((f32[4,4,16,256]{3,2,1,0:T(8,128)S(1)}, f32[4,4,16,256]{3,2,1,0:T(8,128)S(1)}, u32[]{:S(2)}, u32[]{:S(2)}) %collective-permute-start.7) | collective-permute-done | bytes 262176 | tf_op jit(solution)/shard_map/ppermute | solution.py:396
  52.1 1.7 %collective-permute-start.8 = (f32[2,4,16,256]{3,2,1,0:T(8,128)S(1)}, f32[2,4,16,256]{3,2,1,0:T(8,128)S(1)}, u32[]{:S(2)}, u32[]{:S(2)}) collective-permute-start(f32[2,4,16,256]{3,2,1,0:T(8,128)S(1)} %get-tuple-element.23), channel_id=1, source_target_pairs={{0,1},{1,0},{2,3},{3,2},{4,5},{5,4},{6,7},{7,6},{8,9},{9,8},{10,11... | collective-permute-start | bytes 393224 | tf_op jit(solution)/shard_map/ppermute | solution.py:396
  53.7 0.0 collective-permute-done.3
  53.7 0.2 collective-permute-start.4
  53.9 3.2 %collective-permute-done.8 = f32[2,4,16,256]{3,2,1,0:T(8,128)S(1)} collective-permute-done((f32[2,4,16,256]{3,2,1,0:T(8,128)S(1)}, f32[2,4,16,256]{3,2,1,0:T(8,128)S(1)}, u32[]{:S(2)}, u32[]{:S(2)}) %collective-permute-start.8) | collective-permute-done | bytes 131104 | tf_op jit(solution)/shard_map/ppermute | solution.py:396
  57.1 0.2 collective-permute-start.9
  57.3 0.8 collective-permute-done.4
  58.1 3.4 %collective-permute-done.9 = f32[1,4,16,256]{3,2,1,0:T(8,128)S(1)} collective-permute-done((f32[1,4,16,256]{3,2,1,0:T(8,128)S(1)}, f32[1,4,16,256]{3,2,1,0:T(8,128)S(1)}, u32[]{:S(2)}, u32[]{:S(2)}) %collective-permute-start.9) | collective-permute-done | bytes 65568 | tf_op jit(solution)/shard_map/ppermute | solution.py:396
  61.5 3.1 %collective-permute-start.10 = (f32[4,16,256]{2,1,0:T(8,128)S(1)}, f32[4,16,256]{2,1,0:T(8,128)S(1)}, u32[]{:S(2)}, u32[]{:S(2)}) collective-permute-start(f32[4,16,256]{2,1,0:T(8,128)S(1)} %select_bitcast_fusion), channel_id=1, source_target_pairs={{0,3},{1,2},{2,1},{3,0},{4,7},{5,6},{6,5},{7,4},{8,11},{9,10},{10,... | collective-permute-start | bytes 196616 | tf_op jit(solution)/shard_map/ppermute | solution.py:396
  64.6 2.5 %collective-permute-done.10 = f32[4,16,256]{2,1,0:T(8,128)S(1)} collective-permute-done((f32[4,16,256]{2,1,0:T(8,128)S(1)}, f32[4,16,256]{2,1,0:T(8,128)S(1)}, u32[]{:S(2)}, u32[]{:S(2)}) %collective-permute-start.10) | collective-permute-done | bytes 65568 | tf_op jit(solution)/shard_map/ppermute | solution.py:396
  67.1 5.5 %collective-permute-start.13 = (f32[4,16,256]{2,1,0:T(8,128)S(1)}, f32[4,16,256]{2,1,0:T(8,128)S(1)}, u32[]{:S(2)}, u32[]{:S(2)}) collective-permute-start(f32[4,16,256]{2,1,0:T(8,128)S(1)} %bitcast_add_fusion), channel_id=1, source_target_pairs={{0,12},{4,8},{8,4},{12,0},{1,13},{5,9},{9,5},{13,1},{2,14},{6,10},... | collective-permute-start | bytes 196616 | tf_op jit(solution)/shard_map/ppermute | solution.py:396
  72.6 1.4 %collective-permute-start.12 = (f32[4,16,256]{2,1,0:T(8,128)S(1)}, f32[4,16,256]{2,1,0:T(8,128)S(1)}, u32[]{:S(2)}, u32[]{:S(2)}) collective-permute-start(f32[4,16,256]{2,1,0:T(8,128)S(1)} %bitcast_add_fusion), channel_id=1, source_target_pairs={{0,8},{4,12},{8,0},{12,4},{1,9},{5,13},{9,1},{13,5},{2,10},{6,14},... | collective-permute-start | bytes 196616 | tf_op jit(solution)/shard_map/ppermute | solution.py:396
  74.0 1.0 %collective-permute-start.11 = (f32[4,16,256]{2,1,0:T(8,128)S(1)}, f32[4,16,256]{2,1,0:T(8,128)S(1)}, u32[]{:S(2)}, u32[]{:S(2)}) collective-permute-start(f32[4,16,256]{2,1,0:T(8,128)S(1)} %bitcast_add_fusion), channel_id=1, source_target_pairs={{0,4},{4,0},{8,12},{12,8},{1,5},{5,1},{9,13},{13,9},{2,6},{6,2},{1... | collective-permute-start | bytes 196616 | tf_op jit(solution)/shard_map/ppermute | solution.py:396
  75.1 0.5 collective-permute-done.13
  75.5 5.2 %collective-permute-done.12 = f32[4,16,256]{2,1,0:T(8,128)S(1)} collective-permute-done((f32[4,16,256]{2,1,0:T(8,128)S(1)}, f32[4,16,256]{2,1,0:T(8,128)S(1)}, u32[]{:S(2)}, u32[]{:S(2)}) %collective-permute-start.12) | collective-permute-done | bytes 65568 | tf_op jit(solution)/shard_map/ppermute | solution.py:396
  80.8 0.0 collective-permute-done.11
  80.8 0.6 slice_bitcast_fusion
  (7 shorter events, 0.2 us)
Async XLA Ops:
  22.2 4.2 %collective-permute-start = (f32[16,4,16,256]{3,2,1,0:T(8,128)S(1)}, f32[16,4,16,256]{3,2,1,0:T(8,128)S(1)}, u32[]{:S(2)}, u32[]{:S(2)}) collective-permute-start(f32[16,4,16,256]{3,2,1,0:T(8,128)S(1)} %get-tuple-element.9), channel_id=1, source_target_pairs={{0,16},{16,0},{32,48},{48,32},{64,80},{80,64},{96,112},{112,96},{1... | collective-permute-start | bytes 3145736 | tf_op jit(solution)/shard_map/ppermute | solution.py:396
  25.8 2.9 %collective-permute-start.5 = (f32[16,4,16,256]{3,2,1,0:T(8,128)S(1)}, f32[16,4,16,256]{3,2,1,0:T(8,128)S(1)}, u32[]{:S(2)}, u32[]{:S(2)}) collective-permute-start(f32[16,4,16,256]{3,2,1,0:T(8,128)S(1)} %get-tuple-element.13), channel_id=1, source_target_pairs={{0,16},{16,0},{32,48},{48,32},{64,80},{80,64},{96,112},{112,96},{1... | collective-permute-start | bytes 3145736 | tf_op jit(solution)/shard_map/ppermute | solution.py:396
  26.6 9.3 %collective-permute-start.1 = (f32[8,4,16,256]{3,2,1,0:T(8,128)S(1)}, f32[8,4,16,256]{3,2,1,0:T(8,128)S(1)}, u32[]{:S(2)}, u32[]{:S(2)}) collective-permute-start(f32[8,4,16,256]{3,2,1,0:T(8,128)S(1)} %get-tuple-element.17), channel_id=1, source_target_pairs={{0,64},{16,208},{32,96},{48,240},{64,0},{80,144},{96,32},{112,176}... | collective-permute-start | bytes 1572872 | tf_op jit(solution)/shard_map/ppermute | solution.py:396
  28.9 15.4 %collective-permute-start.6 = (f32[8,4,16,256]{3,2,1,0:T(8,128)S(1)}, f32[8,4,16,256]{3,2,1,0:T(8,128)S(1)}, u32[]{:S(2)}, u32[]{:S(2)}) collective-permute-start(f32[8,4,16,256]{3,2,1,0:T(8,128)S(1)} %get-tuple-element.15), channel_id=1, source_target_pairs={{0,64},{16,208},{32,96},{48,240},{64,0},{80,144},{96,32},{112,176}... | collective-permute-start | bytes 1572872 | tf_op jit(solution)/shard_map/ppermute | solution.py:396
  36.0 8.9 %collective-permute-start.2 = (f32[4,4,16,256]{3,2,1,0:T(8,128)S(1)}, f32[4,4,16,256]{3,2,1,0:T(8,128)S(1)}, u32[]{:S(2)}, u32[]{:S(2)}) collective-permute-start(f32[4,4,16,256]{3,2,1,0:T(8,128)S(1)} %get-tuple-element.21), channel_id=1, source_target_pairs={{0,192},{16,80},{32,224},{48,112},{64,128},{80,16},{96,160},{112,4... | collective-permute-start | bytes 786440 | tf_op jit(solution)/shard_map/ppermute | solution.py:396
  44.4 7.7 %collective-permute-start.7 = (f32[4,4,16,256]{3,2,1,0:T(8,128)S(1)}, f32[4,4,16,256]{3,2,1,0:T(8,128)S(1)}, u32[]{:S(2)}, u32[]{:S(2)}) collective-permute-start(f32[4,4,16,256]{3,2,1,0:T(8,128)S(1)} %get-tuple-element.19), channel_id=1, source_target_pairs={{0,192},{16,80},{32,224},{48,112},{64,128},{80,16},{96,160},{112,4... | collective-permute-start | bytes 786440 | tf_op jit(solution)/shard_map/ppermute | solution.py:396
  45.0 8.8 %collective-permute-start.3 = (f32[2,4,16,256]{3,2,1,0:T(8,128)S(1)}, f32[2,4,16,256]{3,2,1,0:T(8,128)S(1)}, u32[]{:S(2)}, u32[]{:S(2)}) collective-permute-start(f32[2,4,16,256]{3,2,1,0:T(8,128)S(1)} %get-tuple-element.25), channel_id=1, source_target_pairs={{0,1},{1,0},{2,3},{3,2},{4,5},{5,4},{6,7},{7,6},{8,9},{9,8},{10,11... | collective-permute-start | bytes 393224 | tf_op jit(solution)/shard_map/ppermute | solution.py:396
  52.1 5.1 %collective-permute-start.8 = (f32[2,4,16,256]{3,2,1,0:T(8,128)S(1)}, f32[2,4,16,256]{3,2,1,0:T(8,128)S(1)}, u32[]{:S(2)}, u32[]{:S(2)}) collective-permute-start(f32[2,4,16,256]{3,2,1,0:T(8,128)S(1)} %get-tuple-element.23), channel_id=1, source_target_pairs={{0,1},{1,0},{2,3},{3,2},{4,5},{5,4},{6,7},{7,6},{8,9},{9,8},{10,11... | collective-permute-start | bytes 393224 | tf_op jit(solution)/shard_map/ppermute | solution.py:396
  53.7 4.4 %collective-permute-start.4 = (f32[1,4,16,256]{3,2,1,0:T(8,128)S(1)}, f32[1,4,16,256]{3,2,1,0:T(8,128)S(1)}, u32[]{:S(2)}, u32[]{:S(2)}) collective-permute-start(f32[1,4,16,256]{3,2,1,0:T(8,128)S(1)} %slice_add_fusion.14), channel_id=1, source_target_pairs={{0,32},{16,48},{32,0},{48,16},{64,96},{80,112},{96,64},{112,80},{1... | collective-permute-start | bytes 196616 | tf_op jit(solution)/shard_map/ppermute | solution.py:396
  57.1 4.4 %collective-permute-start.9 = (f32[1,4,16,256]{3,2,1,0:T(8,128)S(1)}, f32[1,4,16,256]{3,2,1,0:T(8,128)S(1)}, u32[]{:S(2)}, u32[]{:S(2)}) collective-permute-start(f32[1,4,16,256]{3,2,1,0:T(8,128)S(1)} %slice_add_fusion.12), channel_id=1, source_target_pairs={{0,32},{16,48},{32,0},{48,16},{64,96},{80,112},{96,64},{112,80},{1... | collective-permute-start | bytes 196616 | tf_op jit(solution)/shard_map/ppermute | solution.py:396
  61.5 5.6 %collective-permute-start.10 = (f32[4,16,256]{2,1,0:T(8,128)S(1)}, f32[4,16,256]{2,1,0:T(8,128)S(1)}, u32[]{:S(2)}, u32[]{:S(2)}) collective-permute-start(f32[4,16,256]{2,1,0:T(8,128)S(1)} %select_bitcast_fusion), channel_id=1, source_target_pairs={{0,3},{1,2},{2,1},{3,0},{4,7},{5,6},{6,5},{7,4},{8,11},{9,10},{10,... | collective-permute-start | bytes 196616 | tf_op jit(solution)/shard_map/ppermute | solution.py:396
  67.1 8.4 %collective-permute-start.13 = (f32[4,16,256]{2,1,0:T(8,128)S(1)}, f32[4,16,256]{2,1,0:T(8,128)S(1)}, u32[]{:S(2)}, u32[]{:S(2)}) collective-permute-start(f32[4,16,256]{2,1,0:T(8,128)S(1)} %bitcast_add_fusion), channel_id=1, source_target_pairs={{0,12},{4,8},{8,4},{12,0},{1,13},{5,9},{9,5},{13,1},{2,14},{6,10},... | collective-permute-start | bytes 196616 | tf_op jit(solution)/shard_map/ppermute | solution.py:396
  72.6 8.2 %collective-permute-start.12 = (f32[4,16,256]{2,1,0:T(8,128)S(1)}, f32[4,16,256]{2,1,0:T(8,128)S(1)}, u32[]{:S(2)}, u32[]{:S(2)}) collective-permute-start(f32[4,16,256]{2,1,0:T(8,128)S(1)} %bitcast_add_fusion), channel_id=1, source_target_pairs={{0,8},{4,12},{8,0},{12,4},{1,9},{5,13},{9,1},{13,5},{2,10},{6,14},... | collective-permute-start | bytes 196616 | tf_op jit(solution)/shard_map/ppermute | solution.py:396
  74.0 6.7 %collective-permute-start.11 = (f32[4,16,256]{2,1,0:T(8,128)S(1)}, f32[4,16,256]{2,1,0:T(8,128)S(1)}, u32[]{:S(2)}, u32[]{:S(2)}) collective-permute-start(f32[4,16,256]{2,1,0:T(8,128)S(1)} %bitcast_add_fusion), channel_id=1, source_target_pairs={{0,4},{4,0},{8,12},{12,8},{1,5},{5,1},{9,13},{13,9},{2,6},{6,2},{1... | collective-permute-start | bytes 196616 | tf_op jit(solution)/shard_map/ppermute | solution.py:396

commit v2 on v1

--- a/solution.py
+++ b/solution.py
@@ -4,6 +4,7 @@
 from jax.experimental import pallas as pl
 from jax.experimental.pallas import tpu as pltpu
 from jax.sharding import PartitionSpec as P
+
 
 N = 256
 CH = 32
@@ -88,12 +89,15 @@
     where_y = lax.axis_index("layer")
     y_at = (layer ^ (layer >> 1) ^ where_y ^ (where_y >> 1)) & 1
     for core_at, to in ((0, keep), (1, send)):
+        turn = core ^ core_at
         for x_at in range(4):
-            x_from = my_x ^ step_of(x_at, core ^ core_at)
+            x_from = my_x ^ step_of(x_at, turn)
             for z_at in range(2):
-                chunk = x_from * 4 + (my_z ^ z_at) * 2 + (core ^ core_at)
+                chunk = x_from * 4 + (my_z ^ z_at) * 2 + turn
+                other = y_at * (2 - turn) + z_at * (1 + turn)
+                spot = x_at * 4 + other if layer >= 2 else other * 4 + x_at
                 for comp in range(4):
-                    to[x_at * 4 + y_at * 2 + z_at, comp] = done[comp, chunk]
+                    to[spot, comp] = done[comp, chunk]
 
 
 def back_products(m, i, weight, done):
@@ -217,7 +221,7 @@
 
         pieces(post)
 
-    def square(i):
+    def square():
         def post(r, a, b, c):
             m.store("sr", r, a - b)
             m.store("si", r, c - a - b)
@@ -282,7 +286,7 @@
 
     blocks[0].wait()
     scale(0)
-    square(0)
+    square()
     hops.wait()
     for i in range(4):
         pieces(lambda r, x: m.put(f"V{i}", r, x), coup[kind[i]])
@@ -295,7 +299,7 @@
             dressed(i - 1)
         scale(i)
         lesser(i - 1)
-        square(i)
+        square()
         lesser_turned(i - 1)
         green(i)
         lesser_hop(i - 1)
@@ -321,15 +325,20 @@
     hand_out(2, done, keep, send)
 
 
-def backward_kernel(kept_pairs, kept_full, keep, send, pairs, full, done):
+def third_kernel(kept_pairs, kept_full, next_pair, done, pairs, full):
     m = Parts(pairs, full, kept_pairs, kept_full)
-    weight = kept_full[KEPT_FULL.index("weight"), 0:1, :]
-    for i in (1, 0):
-        bond, density, report, _, _ = back_products(m, i, weight, done)
-        bond()
-        density()
-        report()
-        hand_out(i, done, keep, send)
+    m.kept["W1"] = (next_pair, 0)
+    for step in back_products(m, 1, kept_full[KEPT_FULL.index("weight"), 0:1, :], done)[:3]:
+        step()
+
+
+def last_kernel(kept_pairs, kept_full, next_pair, done_before, keep, send, pairs, full, done):
+    m = Parts(pairs, full, kept_pairs, kept_full)
+    m.kept["W1"] = (next_pair, 0)
+    hand_out(1, done_before, keep, send)
+    for step in back_products(m, 0, kept_full[KEPT_FULL.index("weight"), 0:1, :], done)[:3]:
+        step()
+    hand_out(0, done, keep, send)
 
 
 def cost(products):
@@ -372,21 +381,34 @@
     )(*arrays[:4], *[pltpu.with_memory_space_constraint(a, pltpu.HBM) for a in arrays[4:]])
 
 
-def backward(kept_pairs, kept_full):
+def third(kept_pairs, kept_full):
     vmem = pl.BlockSpec(memory_space=pltpu.VMEM)
     return pl.pallas_call(
-        backward_kernel,
-        out_shape=(jax.ShapeDtypeStruct(BLOCK, f32), jax.ShapeDtypeStruct(BLOCK, f32)),
+        third_kernel,
+        out_shape=(jax.ShapeDtypeStruct((1, 2, N, N), bf16), jax.ShapeDtypeStruct((4, 16, 16, N), f32)),
         in_specs=[vmem] * 2,
         out_specs=(vmem,) * 2,
+        scratch_shapes=[pltpu.VMEM((3, 2, N, N), bf16), pltpu.VMEM((1, N, N), f32)],
+        compiler_params=pltpu.CompilerParams(vmem_limit_bytes=12 * 1024 * 1024),
+        cost_estimate=cost(12),
+    )(kept_pairs, kept_full)
+
+
+def last(kept_pairs, kept_full, next_pair, done_before):
+    vmem = pl.BlockSpec(memory_space=pltpu.VMEM)
+    return pl.pallas_call(
+        last_kernel,
+        out_shape=(jax.ShapeDtypeStruct(BLOCK, f32), jax.ShapeDtypeStruct(BLOCK, f32)),
+        in_specs=[vmem] * 4,
+        out_specs=(vmem,) * 2,
         scratch_shapes=[
-            pltpu.VMEM((4, 2, N, N), bf16),
-            pltpu.VMEM((2, N, N), f32),
+            pltpu.VMEM((3, 2, N, N), bf16),
+            pltpu.VMEM((1, N, N), f32),
             pltpu.VMEM((4, 16, 16, N), f32),
         ],
         compiler_params=pltpu.CompilerParams(vmem_limit_bytes=12 * 1024 * 1024),
-        cost_estimate=cost(24),
-    )(kept_pairs, kept_full)
+        cost_estimate=cost(12),
+    )(kept_pairs, kept_full, next_pair, done_before)
 
 
 def swapped(x, axes, partner):
@@ -408,18 +430,13 @@
     return swapped(x, ("layer",), lambda i: i ^ step)
 
 
-def over_z(x):
-    return swapped(x, ("energy",), lambda i: i ^ 2)
-
-
-def to_one_block(keep, got):
-    mine, other = keep, got
-    count = 16
-    for across in (lambda x: over_x(x, 0), lambda x: over_x(x, 1), lambda x: over_y(x, 1), over_z):
-        count //= 2
-        away = mine[count:] + other[count:]
-        mine, other = mine[:count] + other[:count], across(away)
-    return mine[0] + other[0]
+def over_rest(x, turn):
+    return swapped(x, ("energy", "layer"), lambda i: i ^ (8 if ((i >> 2) & 1) ^ turn else 1))
+
+
+def halves(mine, other):
+    count = mine.shape[0] // 2
+    return mine[:count] + other[:count], mine[count:] + other[count:]
 
 
 def per_device(energies, momenta, energy_level, momentum_level, energy_table, momentum_table, onsite, broad, kdiag, fermi, couplings, bond_kind):
@@ -427,15 +444,25 @@
         (energies, momenta, energy_level, momentum_level, energy_table, momentum_table, fermi, bond_kind, broad, kdiag, onsite, couplings)
     )
     got_high = over_core(send_high)
-    keep_low, send_low = backward(kept_pairs, kept_full)
-    got_low = over_core(send_low)
-    high = to_one_block(keep_high, got_high)
-    low = to_one_block(keep_low, got_low)
+    next_pair, done = third(kept_pairs, kept_full)
+    high, away_high = halves(keep_high, got_high)
+    high, away_high, next_pair, done = lax.optimization_barrier((high, away_high, next_pair, done))
+    got_high = over_x(away_high, 0)
+    keep_low, send_low = last(kept_pairs, kept_full, next_pair, done)
+    low, got_low = keep_low, over_core(send_low)
+    for step in range(4):
+        if step:
+            high, away_high = halves(high, got_high)
+            got_high = over_x(away_high, 1) if step == 1 else over_rest(away_high, step - 2)
+        low, away_low = halves(low, got_low)
+        got_low = over_rest(away_low, step) if step < 2 else over_x(away_low, step - 2)
+    high = high[0] + got_high[0]
+    low = low[0] + got_low[0]
     upper = lax.axis_index("layer") >= 2
     got = over_y(jnp.where(upper, low, high), 3)
     mine = jnp.where(upper, high, low) + got
-    near, far, last = (swapped(mine, ("kpt",), lambda i, s=s: i ^ s) for s in (1, 2, 3))
-    total = (mine + near) + (far + last)
+    near, far, both = (swapped(mine, ("kpt",), lambda i, s=s: i ^ s) for s in (1, 2, 3))
+    total = (mine + near) + (far + both)
     return total[None, :2], total[None, 2:]
 
 

time: 82.7 us -> 78 us (0.943)
  waiting for transfers between devices: 35.9 us -> 30.5 us
    ppermute x14, waiting for transfers between devices: 35.9 us -> 30.5 us  [swapped(): return lax.ppermute(x, axes, [(i, partner(i)) for i in range(count)])]
    pallas_call x1 -> x2, Pallas kernels: 3.48 us -> 3.61 us  [the longest x1 1.86 us: last(): pl.pallas_call(last_kernel, out_shape=(jax.ShapeDtypeStruct(BLOCK, f32),...]
  transfers between devices with their start and end apart: 14 -> 14, of which waited for: 10 -> 13; matrix products, arithmetic and copies ran while one was open for 1% -> 1% of each run, Pallas kernels for 4% -> 2%
where the time goes in v2:
time: 78 us; the launch traced here: 76.9 us
  waiting for transfers between devices  30.5 us (39%)
  Pallas kernels  22.6 us (29%)
  starting transfers between devices  19.1 us (24%)
  between operations  3.3 us (4%)
    ppermute x14, waiting for transfers between devices, swapped(): return lax.ppermute(x, axes, [(i, partner(i)) for i in range(count)])  30.5 us
    ppermute x14, starting transfers between devices, swapped(): return lax.ppermute(x, axes, [(i, partner(i)) for i in range(count)])  19.1 us
    pallas_call x1, Pallas kernels, forward(): pl.pallas_call(forward_kernel, out_shape=(jax.ShapeDtypeStruct(BLOCK, f32...  19 us
    pallas_call x1, Pallas kernels, last(): pl.pallas_call(last_kernel, out_shape=(jax.ShapeDtypeStruct(BLOCK, f32),...  1.86 us
    pallas_call x1, Pallas kernels, third(): pl.pallas_call(third_kernel, out_shape=(jax.ShapeDtypeStruct((1, 2, N, N)...  1.75 us
  transfers between devices with their start and end apart: 14, of which 13 were waited for; matrix products, arithmetic and copies ran while one was open for 1% of the time, Pallas kernels for 2%

profile of v2, /device:TPU:38, one launch (start us, length us, event | category | flops | bytes accessed | tf_op | source)
XLA Modules:
  0.0 76.9 jit_solution(8098714134262232697)
XLA Ops:
  3.2 19.0 %shard_map.131 = (f32[16,4,16,256]{3,2,1,0:T(8,128)S(1)}, f32[16,4,16,256]{3,2,1,0:T(8,128)S(1)}, bf16[13,2,256,256]{3,2,1,0:T(8,128)(2,1)S(1)}, f32[3,256,256]{2,1,0:T(8,128)S(1)}) custom-call(f32[1]{0:T(128)S(6)} %copy.14.refs_0_, f32[1]{0:T(128)S(6)} %copy.15.refs_1_, s32[1]{0:T(128)S(6)} %copy.16.refs_2_, s32[1]{0:T(128)S(6)} %copy.17.refs_3_, ...), custom_call_target="tpu_custom_call" | custom-call | flops 13287555072 | bytes 8388608 | tf_op jit(solution)/shard_map/pallas_call | solution.py:355
  22.2 0.1 collective-permute-start
  22.3 1.8 %shard_map.132 = (bf16[1,2,256,256]{3,2,1,0:T(8,128)(2,1)S(1)}, f32[4,16,16,256]{3,2,1,0:T(8,128)S(1)}) custom-call(bf16[13,2,256,256]{3,2,1,0:T(8,128)(2,1)S(1)} %get-tuple-element.16.kept_pairs, f32[3,256,256]{2,1,0:T(8,128)S(1)} %get-tuple-element.17.kept_full), custom_call_target="tpu_custom_call" | custom-call | flops 1207959552 | bytes 8388608 | tf_op jit(solution)/shard_map/pallas_call | solution.py:386
  24.1 0.9 %collective-permute-done = f32[16,4,16,256]{3,2,1,0:T(8,128)S(1)} collective-permute-done((f32[16,4,16,256]{3,2,1,0:T(8,128)S(1)}, f32[16,4,16,256]{3,2,1,0:T(8,128)S(1)}, u32[]{:S(2)}, u32[]{:S(2)}) %collective-permute-start) | collective-permute-done | bytes 1048608 | tf_op jit(solution)/shard_map/ppermute | solution.py:418
  24.9 0.2 slice_add_fusion.2
  25.2 1.9 %shard_map.133 = (f32[16,4,16,256]{3,2,1,0:T(8,128)S(1)}, f32[16,4,16,256]{3,2,1,0:T(8,128)S(1)}) custom-call(bf16[13,2,256,256]{3,2,1,0:T(8,128)(2,1)S(1)} %get-tuple-element.16.kept_pairs, f32[3,256,256]{2,1,0:T(8,128)S(1)} %get-tuple-element.17.kept_full, bf16[1,2,256,256]{3,2,1,0:T(8,128)(2,1)S(1)} %get-tuple-element.22.next_pair, ...), custom_call_target="tpu_custom_call" | custom-call | flops 1207959552 | bytes 8388608 | tf_op jit(solution)/shard_map/pallas_call | solution.py:399
  27.0 0.2 collective-permute-start.5
  27.2 0.8 %collective-permute-start.1 = (f32[8,4,16,256]{3,2,1,0:T(8,128)S(1)}, f32[8,4,16,256]{3,2,1,0:T(8,128)S(1)}, u32[]{:S(2)}, u32[]{:S(2)}) collective-permute-start(f32[8,4,16,256]{3,2,1,0:T(8,128)S(1)} %get-tuple-element.21), channel_id=1, source_target_pairs={{0,64},{16,208},{32,96},{48,240},{64,0},{80,144},{96,32},{112,176}... | collective-permute-start | bytes 1572872 | tf_op jit(solution)/shard_map/ppermute | solution.py:418
  28.1 1.7 %collective-permute-done.5 = f32[16,4,16,256]{3,2,1,0:T(8,128)S(1)} collective-permute-done((f32[16,4,16,256]{3,2,1,0:T(8,128)S(1)}, f32[16,4,16,256]{3,2,1,0:T(8,128)S(1)}, u32[]{:S(2)}, u32[]{:S(2)}) %collective-permute-start.5) | collective-permute-done | bytes 1048608 | tf_op jit(solution)/shard_map/ppermute | solution.py:418
  29.8 0.2 slice_add_fusion.1
  30.0 1.7 %collective-permute-start.6 = (f32[8,4,16,256]{3,2,1,0:T(8,128)S(1)}, f32[8,4,16,256]{3,2,1,0:T(8,128)S(1)}, u32[]{:S(2)}, u32[]{:S(2)}) collective-permute-start(f32[8,4,16,256]{3,2,1,0:T(8,128)S(1)} %get-tuple-element.27), channel_id=1, source_target_pairs={{0,1},{1,0},{2,3},{3,2},{16,48},{17,49},{18,50},{19,51},{32,33},{3... | collective-permute-start | bytes 1572872 | tf_op jit(solution)/shard_map/ppermute | solution.py:418
  31.6 4.8 %collective-permute-done.1 = f32[8,4,16,256]{3,2,1,0:T(8,128)S(1)} collective-permute-done((f32[8,4,16,256]{3,2,1,0:T(8,128)S(1)}, f32[8,4,16,256]{3,2,1,0:T(8,128)S(1)}, u32[]{:S(2)}, u32[]{:S(2)}) %collective-permute-start.1) | collective-permute-done | bytes 524320 | tf_op jit(solution)/shard_map/ppermute | solution.py:418
  36.4 0.1 slice_add_fusion.7
  36.5 0.6 collective-permute-start.2
  37.1 2.2 %collective-permute-done.6 = f32[8,4,16,256]{3,2,1,0:T(8,128)S(1)} collective-permute-done((f32[8,4,16,256]{3,2,1,0:T(8,128)S(1)}, f32[8,4,16,256]{3,2,1,0:T(8,128)S(1)}, u32[]{:S(2)}, u32[]{:S(2)}) %collective-permute-start.6) | collective-permute-done | bytes 524320 | tf_op jit(solution)/shard_map/ppermute | solution.py:418
  39.3 0.1 slice_add_fusion.5
  39.3 0.2 collective-permute-start.7
  39.5 4.7 %collective-permute-done.2 = f32[4,4,16,256]{3,2,1,0:T(8,128)S(1)} collective-permute-done((f32[4,4,16,256]{3,2,1,0:T(8,128)S(1)}, f32[4,4,16,256]{3,2,1,0:T(8,128)S(1)}, u32[]{:S(2)}, u32[]{:S(2)}) %collective-permute-start.2) | collective-permute-done | bytes 262176 | tf_op jit(solution)/shard_map/ppermute | solution.py:418
  44.2 1.7 %collective-permute-start.3 = (f32[2,4,16,256]{3,2,1,0:T(8,128)S(1)}, f32[2,4,16,256]{3,2,1,0:T(8,128)S(1)}, u32[]{:S(2)}, u32[]{:S(2)}) collective-permute-start(f32[2,4,16,256]{3,2,1,0:T(8,128)S(1)} %get-tuple-element.37), channel_id=1, source_target_pairs={{0,1},{1,0},{2,3},{3,2},{16,48},{17,49},{18,50},{19,51},{32,33},{3... | collective-permute-start | bytes 393224 | tf_op jit(solution)/shard_map/ppermute | solution.py:418
  45.9 0.4 collective-permute-done.7
  46.4 1.4 %collective-permute-start.8 = (f32[2,4,16,256]{3,2,1,0:T(8,128)S(1)}, f32[2,4,16,256]{3,2,1,0:T(8,128)S(1)}, u32[]{:S(2)}, u32[]{:S(2)}) collective-permute-start(f32[2,4,16,256]{3,2,1,0:T(8,128)S(1)} %get-tuple-element.35), channel_id=1, source_target_pairs={{0,64},{16,208},{32,96},{48,240},{64,0},{80,144},{96,32},{112,176}... | collective-permute-start | bytes 393224 | tf_op jit(solution)/shard_map/ppermute | solution.py:418
  47.8 1.5 %collective-permute-done.3 = f32[2,4,16,256]{3,2,1,0:T(8,128)S(1)} collective-permute-done((f32[2,4,16,256]{3,2,1,0:T(8,128)S(1)}, f32[2,4,16,256]{3,2,1,0:T(8,128)S(1)}, u32[]{:S(2)}, u32[]{:S(2)}) %collective-permute-start.3) | collective-permute-done | bytes 131104 | tf_op jit(solution)/shard_map/ppermute | solution.py:418
  49.3 0.2 collective-permute-start.4
  49.5 1.9 %collective-permute-done.8 = f32[2,4,16,256]{3,2,1,0:T(8,128)S(1)} collective-permute-done((f32[2,4,16,256]{3,2,1,0:T(8,128)S(1)}, f32[2,4,16,256]{3,2,1,0:T(8,128)S(1)}, u32[]{:S(2)}, u32[]{:S(2)}) %collective-permute-start.8) | collective-permute-done | bytes 131104 | tf_op jit(solution)/shard_map/ppermute | solution.py:418
  51.4 1.4 %collective-permute-start.9 = (f32[1,4,16,256]{3,2,1,0:T(8,128)S(1)}, f32[1,4,16,256]{3,2,1,0:T(8,128)S(1)}, u32[]{:S(2)}, u32[]{:S(2)}) collective-permute-start(f32[1,4,16,256]{3,2,1,0:T(8,128)S(1)} %slice_add_fusion.12), channel_id=1, source_target_pairs={{0,192},{16,80},{32,224},{48,112},{64,128},{80,16},{96,160},{112,4... | collective-permute-start | bytes 196616 | tf_op jit(solution)/shard_map/ppermute | solution.py:418
  52.8 0.8 %collective-permute-done.4 = f32[1,4,16,256]{3,2,1,0:T(8,128)S(1)} collective-permute-done((f32[1,4,16,256]{3,2,1,0:T(8,128)S(1)}, f32[1,4,16,256]{3,2,1,0:T(8,128)S(1)}, u32[]{:S(2)}, u32[]{:S(2)}) %collective-permute-start.4) | collective-permute-done | bytes 65568 | tf_op jit(solution)/shard_map/ppermute | solution.py:418
  53.6 3.6 %collective-permute-done.9 = f32[1,4,16,256]{3,2,1,0:T(8,128)S(1)} collective-permute-done((f32[1,4,16,256]{3,2,1,0:T(8,128)S(1)}, f32[1,4,16,256]{3,2,1,0:T(8,128)S(1)}, u32[]{:S(2)}, u32[]{:S(2)}) %collective-permute-start.9) | collective-permute-done | bytes 65568 | tf_op jit(solution)/shard_map/ppermute | solution.py:418
  57.2 3.1 %collective-permute-start.10 = (f32[4,16,256]{2,1,0:T(8,128)S(1)}, f32[4,16,256]{2,1,0:T(8,128)S(1)}, u32[]{:S(2)}, u32[]{:S(2)}) collective-permute-start(f32[4,16,256]{2,1,0:T(8,128)S(1)} %select_bitcast_fusion), channel_id=1, source_target_pairs={{0,3},{1,2},{2,1},{3,0},{4,7},{5,6},{6,5},{7,4},{8,11},{9,10},{10,... | collective-permute-start | bytes 196616 | tf_op jit(solution)/shard_map/ppermute | solution.py:418
  60.3 2.5 %collective-permute-done.10 = f32[4,16,256]{2,1,0:T(8,128)S(1)} collective-permute-done((f32[4,16,256]{2,1,0:T(8,128)S(1)}, f32[4,16,256]{2,1,0:T(8,128)S(1)}, u32[]{:S(2)}, u32[]{:S(2)}) %collective-permute-start.10) | collective-permute-done | bytes 65568 | tf_op jit(solution)/shard_map/ppermute | solution.py:418
  62.8 6.4 %collective-permute-start.12 = (f32[4,16,256]{2,1,0:T(8,128)S(1)}, f32[4,16,256]{2,1,0:T(8,128)S(1)}, u32[]{:S(2)}, u32[]{:S(2)}) collective-permute-start(f32[4,16,256]{2,1,0:T(8,128)S(1)} %bitcast_add_fusion), channel_id=1, source_target_pairs={{0,8},{4,12},{8,0},{12,4},{1,9},{5,13},{9,1},{13,5},{2,10},{6,14},... | collective-permute-start | bytes 196616 | tf_op jit(solution)/shard_map/ppermute | solution.py:418
  69.2 0.5 collective-permute-start.13
  69.8 0.9 %collective-permute-start.11 = (f32[4,16,256]{2,1,0:T(8,128)S(1)}, f32[4,16,256]{2,1,0:T(8,128)S(1)}, u32[]{:S(2)}, u32[]{:S(2)}) collective-permute-start(f32[4,16,256]{2,1,0:T(8,128)S(1)} %bitcast_add_fusion), channel_id=1, source_target_pairs={{0,4},{4,0},{8,12},{12,8},{1,5},{5,1},{9,13},{13,9},{2,6},{6,2},{1... | collective-permute-start | bytes 196616 | tf_op jit(solution)/shard_map/ppermute | solution.py:418
  70.7 1.4 %collective-permute-done.12 = f32[4,16,256]{2,1,0:T(8,128)S(1)} collective-permute-done((f32[4,16,256]{2,1,0:T(8,128)S(1)}, f32[4,16,256]{2,1,0:T(8,128)S(1)}, u32[]{:S(2)}, u32[]{:S(2)}) %collective-permute-start.12) | collective-permute-done | bytes 65568 | tf_op jit(solution)/shard_map/ppermute | solution.py:418
  72.0 4.2 %collective-permute-done.13 = f32[4,16,256]{2,1,0:T(8,128)S(1)} collective-permute-done((f32[4,16,256]{2,1,0:T(8,128)S(1)}, f32[4,16,256]{2,1,0:T(8,128)S(1)}, u32[]{:S(2)}, u32[]{:S(2)}) %collective-permute-start.13) | collective-permute-done | bytes 65568 | tf_op jit(solution)/shard_map/ppermute | solution.py:418
  76.3 0.0 collective-permute-done.11
  76.3 0.6 slice_bitcast_fusion
  (7 shorter events, 0.2 us)
Async XLA Ops:
  22.2 2.7 %collective-permute-start = (f32[16,4,16,256]{3,2,1,0:T(8,128)S(1)}, f32[16,4,16,256]{3,2,1,0:T(8,128)S(1)}, u32[]{:S(2)}, u32[]{:S(2)}) collective-permute-start(f32[16,4,16,256]{3,2,1,0:T(8,128)S(1)} %get-tuple-element.15), channel_id=1, source_target_pairs={{0,16},{16,0},{32,48},{48,32},{64,80},{80,64},{96,112},{112,96},{1... | collective-permute-start | bytes 3145736 | tf_op jit(solution)/shard_map/ppermute | solution.py:418
  27.0 2.7 %collective-permute-start.5 = (f32[16,4,16,256]{3,2,1,0:T(8,128)S(1)}, f32[16,4,16,256]{3,2,1,0:T(8,128)S(1)}, u32[]{:S(2)}, u32[]{:S(2)}) collective-permute-start(f32[16,4,16,256]{3,2,1,0:T(8,128)S(1)} %get-tuple-element.25), channel_id=1, source_target_pairs={{0,16},{16,0},{32,48},{48,32},{64,80},{80,64},{96,112},{112,96},{1... | collective-permute-start | bytes 3145736 | tf_op jit(solution)/shard_map/ppermute | solution.py:418
  27.2 9.2 %collective-permute-start.1 = (f32[8,4,16,256]{3,2,1,0:T(8,128)S(1)}, f32[8,4,16,256]{3,2,1,0:T(8,128)S(1)}, u32[]{:S(2)}, u32[]{:S(2)}) collective-permute-start(f32[8,4,16,256]{3,2,1,0:T(8,128)S(1)} %get-tuple-element.21), channel_id=1, source_target_pairs={{0,64},{16,208},{32,96},{48,240},{64,0},{80,144},{96,32},{112,176}... | collective-permute-start | bytes 1572872 | tf_op jit(solution)/shard_map/ppermute | solution.py:418
  30.0 9.3 %collective-permute-start.6 = (f32[8,4,16,256]{3,2,1,0:T(8,128)S(1)}, f32[8,4,16,256]{3,2,1,0:T(8,128)S(1)}, u32[]{:S(2)}, u32[]{:S(2)}) collective-permute-start(f32[8,4,16,256]{3,2,1,0:T(8,128)S(1)} %get-tuple-element.27), channel_id=1, source_target_pairs={{0,1},{1,0},{2,3},{3,2},{16,48},{17,49},{18,50},{19,51},{32,33},{3... | collective-permute-start | bytes 1572872 | tf_op jit(solution)/shard_map/ppermute | solution.py:418
  36.5 7.7 %collective-permute-start.2 = (f32[4,4,16,256]{3,2,1,0:T(8,128)S(1)}, f32[4,4,16,256]{3,2,1,0:T(8,128)S(1)}, u32[]{:S(2)}, u32[]{:S(2)}) collective-permute-start(f32[4,4,16,256]{3,2,1,0:T(8,128)S(1)} %get-tuple-element.33), channel_id=1, source_target_pairs={{0,192},{16,80},{32,224},{48,112},{64,128},{80,16},{96,160},{112,4... | collective-permute-start | bytes 786440 | tf_op jit(solution)/shard_map/ppermute | solution.py:418
  39.3 7.0 %collective-permute-start.7 = (f32[4,4,16,256]{3,2,1,0:T(8,128)S(1)}, f32[4,4,16,256]{3,2,1,0:T(8,128)S(1)}, u32[]{:S(2)}, u32[]{:S(2)}) collective-permute-start(f32[4,4,16,256]{3,2,1,0:T(8,128)S(1)} %get-tuple-element.31), channel_id=1, source_target_pairs={{0,32},{1,33},{2,34},{3,35},{16,17},{17,16},{18,19},{19,18},{32,0}... | collective-permute-start | bytes 786440 | tf_op jit(solution)/shard_map/ppermute | solution.py:418
  44.2 5.1 %collective-permute-start.3 = (f32[2,4,16,256]{3,2,1,0:T(8,128)S(1)}, f32[2,4,16,256]{3,2,1,0:T(8,128)S(1)}, u32[]{:S(2)}, u32[]{:S(2)}) collective-permute-start(f32[2,4,16,256]{3,2,1,0:T(8,128)S(1)} %get-tuple-element.37), channel_id=1, source_target_pairs={{0,1},{1,0},{2,3},{3,2},{16,48},{17,49},{18,50},{19,51},{32,33},{3... | collective-permute-start | bytes 393224 | tf_op jit(solution)/shard_map/ppermute | solution.py:418
  46.4 5.1 %collective-permute-start.8 = (f32[2,4,16,256]{3,2,1,0:T(8,128)S(1)}, f32[2,4,16,256]{3,2,1,0:T(8,128)S(1)}, u32[]{:S(2)}, u32[]{:S(2)}) collective-permute-start(f32[2,4,16,256]{3,2,1,0:T(8,128)S(1)} %get-tuple-element.35), channel_id=1, source_target_pairs={{0,64},{16,208},{32,96},{48,240},{64,0},{80,144},{96,32},{112,176}... | collective-permute-start | bytes 393224 | tf_op jit(solution)/shard_map/ppermute | solution.py:418
  49.3 4.4 %collective-permute-start.4 = (f32[1,4,16,256]{3,2,1,0:T(8,128)S(1)}, f32[1,4,16,256]{3,2,1,0:T(8,128)S(1)}, u32[]{:S(2)}, u32[]{:S(2)}) collective-permute-start(f32[1,4,16,256]{3,2,1,0:T(8,128)S(1)} %slice_add_fusion.14), channel_id=1, source_target_pairs={{0,32},{1,33},{2,34},{3,35},{16,17},{17,16},{18,19},{19,18},{32,0}... | collective-permute-start | bytes 196616 | tf_op jit(solution)/shard_map/ppermute | solution.py:418
  51.4 5.8 %collective-permute-start.9 = (f32[1,4,16,256]{3,2,1,0:T(8,128)S(1)}, f32[1,4,16,256]{3,2,1,0:T(8,128)S(1)}, u32[]{:S(2)}, u32[]{:S(2)}) collective-permute-start(f32[1,4,16,256]{3,2,1,0:T(8,128)S(1)} %slice_add_fusion.12), channel_id=1, source_target_pairs={{0,192},{16,80},{32,224},{48,112},{64,128},{80,16},{96,160},{112,4... | collective-permute-start | bytes 196616 | tf_op jit(solution)/shard_map/ppermute | solution.py:418
  57.2 5.6 %collective-permute-start.10 = (f32[4,16,256]{2,1,0:T(8,128)S(1)}, f32[4,16,256]{2,1,0:T(8,128)S(1)}, u32[]{:S(2)}, u32[]{:S(2)}) collective-permute-start(f32[4,16,256]{2,1,0:T(8,128)S(1)} %select_bitcast_fusion), channel_id=1, source_target_pairs={{0,3},{1,2},{2,1},{3,0},{4,7},{5,6},{6,5},{7,4},{8,11},{9,10},{10,... | collective-permute-start | bytes 196616 | tf_op jit(solution)/shard_map/ppermute | solution.py:418
  62.8 9.2 %collective-permute-start.12 = (f32[4,16,256]{2,1,0:T(8,128)S(1)}, f32[4,16,256]{2,1,0:T(8,128)S(1)}, u32[]{:S(2)}, u32[]{:S(2)}) collective-permute-start(f32[4,16,256]{2,1,0:T(8,128)S(1)} %bitcast_add_fusion), channel_id=1, source_target_pairs={{0,8},{4,12},{8,0},{12,4},{1,9},{5,13},{9,1},{13,5},{2,10},{6,14},... | collective-permute-start | bytes 196616 | tf_op jit(solution)/shard_map/ppermute | solution.py:418
  69.2 7.1 %collective-permute-start.13 = (f32[4,16,256]{2,1,0:T(8,128)S(1)}, f32[4,16,256]{2,1,0:T(8,128)S(1)}, u32[]{:S(2)}, u32[]{:S(2)}) collective-permute-start(f32[4,16,256]{2,1,0:T(8,128)S(1)} %bitcast_add_fusion), channel_id=1, source_target_pairs={{0,12},{4,8},{8,4},{12,0},{1,13},{5,9},{9,5},{13,1},{2,14},{6,10},... | collective-permute-start | bytes 196616 | tf_op jit(solution)/shard_map/ppermute | solution.py:418
  69.8 6.5 %collective-permute-start.11 = (f32[4,16,256]{2,1,0:T(8,128)S(1)}, f32[4,16,256]{2,1,0:T(8,128)S(1)}, u32[]{:S(2)}, u32[]{:S(2)}) collective-permute-start(f32[4,16,256]{2,1,0:T(8,128)S(1)} %bitcast_add_fusion), channel_id=1, source_target_pairs={{0,4},{4,0},{8,12},{12,8},{1,5},{5,1},{9,13},{13,9},{2,6},{6,2},{1... | collective-permute-start | bytes 196616 | tf_op jit(solution)/shard_map/ppermute | solution.py:418

commit v3 on v2

--- a/solution.py
+++ b/solution.py
@@ -94,8 +94,10 @@
             x_from = my_x ^ step_of(x_at, turn)
             for z_at in range(2):
                 chunk = x_from * 4 + (my_z ^ z_at) * 2 + turn
-                other = y_at * (2 - turn) + z_at * (1 + turn)
-                spot = x_at * 4 + other if layer >= 2 else other * 4 + x_at
+                if layer >= 2:
+                    spot = (y_at * (2 - turn) + z_at * (1 + turn)) * 4 + x_at
+                else:
+                    spot = (x_at >> 1) * 4 + (x_at & 1) * (2 - turn) + z_at * (1 + turn)
                 for comp in range(4):
                     to[spot, comp] = done[comp, chunk]
 
@@ -150,7 +152,7 @@
 
 
 def forward_kernel(*refs):
-    arrays, (keep, send, kept_pairs, kept_full, pairs, full, done), local, sems = refs[4:12], refs[12:19], refs[19:27], refs[27]
+    arrays, (keep, send, kept_pairs, kept_full, sides, pairs, full, done), local, sems = refs[4:12], refs[12:20], refs[20:28], refs[28]
     pe, pk, elev, mlev = refs[:4]
     etab, mtab, fermi, kind, broad, kdiag, onsite, coup = local
     small = [pltpu.make_async_copy(arrays[n], local[n], sems.at[n]) for n in range(6)]
@@ -159,6 +161,9 @@
     for copy in small + blocks[:1] + [hops] + blocks[1:]:
         copy.start()
     m = Parts(pairs, full, kept_pairs, kept_full)
+    where = lax.axis_index("layer")
+    sides[0] = jnp.full((16, N), (((where ^ (where >> 1)) & 1) == 1).astype(f32))
+    sides[1] = jnp.full((16, N), (where >= 2).astype(f32))
     for copy in small:
         copy.wait()
     e = pe[0]
@@ -325,17 +330,17 @@
     hand_out(2, done, keep, send)
 
 
-def third_kernel(kept_pairs, kept_full, next_pair, done, pairs, full):
+def third_kernel(kept_pairs, kept_full, next_pair, keep, send, pairs, full, done):
     m = Parts(pairs, full, kept_pairs, kept_full)
     m.kept["W1"] = (next_pair, 0)
     for step in back_products(m, 1, kept_full[KEPT_FULL.index("weight"), 0:1, :], done)[:3]:
         step()
-
-
-def last_kernel(kept_pairs, kept_full, next_pair, done_before, keep, send, pairs, full, done):
+    hand_out(1, done, keep, send)
+
+
+def last_kernel(kept_pairs, kept_full, next_pair, keep, send, pairs, full, done):
     m = Parts(pairs, full, kept_pairs, kept_full)
     m.kept["W1"] = (next_pair, 0)
-    hand_out(1, done_before, keep, send)
     for step in back_products(m, 0, kept_full[KEPT_FULL.index("weight"), 0:1, :], done)[:3]:
         step()
     hand_out(0, done, keep, send)
@@ -346,6 +351,7 @@
 
 
 BLOCK = (16, 4, 16, N)
+HALF_BLOCK = (8, 4, 16, N)
 
 
 def forward(arrays):
@@ -359,9 +365,10 @@
             jax.ShapeDtypeStruct(BLOCK, f32),
             jax.ShapeDtypeStruct((len(KEPT), 2, N, N), bf16),
             jax.ShapeDtypeStruct((len(KEPT_FULL), N, N), f32),
+            jax.ShapeDtypeStruct((2, 16, N), f32),
         ),
         in_specs=[smem] * 4 + [hbm] * 8,
-        out_specs=(vmem,) * 4,
+        out_specs=(vmem,) * 5,
         scratch_shapes=[
             pltpu.VMEM((56, 2, N, N), bf16),
             pltpu.VMEM((18, N, N), f32),
@@ -376,7 +383,7 @@
             pltpu.VMEM((3, N, N), f32),
             pltpu.SemaphoreType.DMA((12,)),
         ],
-        compiler_params=pltpu.CompilerParams(vmem_limit_bytes=44 * 1024 * 1024),
+        compiler_params=pltpu.CompilerParams(vmem_limit_bytes=32 * 1024 * 1024),
         cost_estimate=cost(132),
     )(*arrays[:4], *[pltpu.with_memory_space_constraint(a, pltpu.HBM) for a in arrays[4:]])
 
@@ -385,21 +392,29 @@
     vmem = pl.BlockSpec(memory_space=pltpu.VMEM)
     return pl.pallas_call(
         third_kernel,
-        out_shape=(jax.ShapeDtypeStruct((1, 2, N, N), bf16), jax.ShapeDtypeStruct((4, 16, 16, N), f32)),
+        out_shape=(
+            jax.ShapeDtypeStruct((1, 2, N, N), bf16),
+            jax.ShapeDtypeStruct(HALF_BLOCK, f32),
+            jax.ShapeDtypeStruct(HALF_BLOCK, f32),
+        ),
         in_specs=[vmem] * 2,
-        out_specs=(vmem,) * 2,
-        scratch_shapes=[pltpu.VMEM((3, 2, N, N), bf16), pltpu.VMEM((1, N, N), f32)],
+        out_specs=(vmem,) * 3,
+        scratch_shapes=[
+            pltpu.VMEM((3, 2, N, N), bf16),
+            pltpu.VMEM((1, N, N), f32),
+            pltpu.VMEM((4, 16, 16, N), f32),
+        ],
         compiler_params=pltpu.CompilerParams(vmem_limit_bytes=12 * 1024 * 1024),
         cost_estimate=cost(12),
     )(kept_pairs, kept_full)
 
 
-def last(kept_pairs, kept_full, next_pair, done_before):
+def last(kept_pairs, kept_full, next_pair):
     vmem = pl.BlockSpec(memory_space=pltpu.VMEM)
     return pl.pallas_call(
         last_kernel,
-        out_shape=(jax.ShapeDtypeStruct(BLOCK, f32), jax.ShapeDtypeStruct(BLOCK, f32)),
-        in_specs=[vmem] * 4,
+        out_shape=(jax.ShapeDtypeStruct(HALF_BLOCK, f32), jax.ShapeDtypeStruct(HALF_BLOCK, f32)),
+        in_specs=[vmem] * 3,
         out_specs=(vmem,) * 2,
         scratch_shapes=[
             pltpu.VMEM((3, 2, N, N), bf16),
@@ -408,7 +423,7 @@
         ],
         compiler_params=pltpu.CompilerParams(vmem_limit_bytes=12 * 1024 * 1024),
         cost_estimate=cost(12),
-    )(kept_pairs, kept_full, next_pair, done_before)
+    )(kept_pairs, kept_full, next_pair)
 
 
 def swapped(x, axes, partner):
@@ -434,31 +449,40 @@
     return swapped(x, ("energy", "layer"), lambda i: i ^ (8 if ((i >> 2) & 1) ^ turn else 1))
 
 
+def over_mixed(x, turn):
+    return swapped(x, ("energy",), lambda i: i ^ ((12, 4)[i & 1] if (i & 1) == turn else 2))
+
+
 def halves(mine, other):
     count = mine.shape[0] // 2
     return mine[:count] + other[:count], mine[count:] + other[count:]
 
 
 def per_device(energies, momenta, energy_level, momentum_level, energy_table, momentum_table, onsite, broad, kdiag, fermi, couplings, bond_kind):
-    keep_high, send_high, kept_pairs, kept_full = forward(
+    keep_high, send_high, kept_pairs, kept_full, sides = forward(
         (energies, momenta, energy_level, momentum_level, energy_table, momentum_table, fermi, bond_kind, broad, kdiag, onsite, couplings)
     )
     got_high = over_core(send_high)
-    next_pair, done = third(kept_pairs, kept_full)
+    next_pair, keep_1, send_1 = third(kept_pairs, kept_full)
     high, away_high = halves(keep_high, got_high)
-    high, away_high, next_pair, done = lax.optimization_barrier((high, away_high, next_pair, done))
-    got_high = over_x(away_high, 0)
-    keep_low, send_low = last(kept_pairs, kept_full, next_pair, done)
-    low, got_low = keep_low, over_core(send_low)
-    for step in range(4):
-        if step:
-            high, away_high = halves(high, got_high)
-            got_high = over_x(away_high, 1) if step == 1 else over_rest(away_high, step - 2)
-        low, away_low = halves(low, got_low)
-        got_low = over_rest(away_low, step) if step < 2 else over_x(away_low, step - 2)
+    high, away_high, next_pair, send_1 = lax.optimization_barrier((high, away_high, next_pair, send_1))
+    got_high = over_rest(away_high, 0)
+    got_1 = over_core(send_1)
+    keep_0, send_0 = last(kept_pairs, kept_full, next_pair)
+    got_0 = over_core(send_0)
+    low_1, low_0 = keep_1, keep_0
+    for step in range(3):
+        low_1, away_1 = halves(low_1, got_1)
+        got_1 = over_mixed(away_1, step - 1) if step else over_x(away_1, 0)
+        low_0, away_0 = halves(low_0, got_0)
+        got_0 = over_mixed(away_0, step - 1) if step else over_x(away_0, 0)
+        high, away_high = halves(high, got_high)
+        got_high = over_x(away_high, step - 1) if step else over_rest(away_high, 1)
     high = high[0] + got_high[0]
-    low = low[0] + got_low[0]
-    upper = lax.axis_index("layer") >= 2
+    low_1 = low_1[0] + got_1[0]
+    low_0 = low_0[0] + got_0[0]
+    odd, upper = sides[0] > 0.5, sides[1] > 0.5
+    low = jnp.where(odd, low_1, low_0) + over_y(jnp.where(odd, low_0, low_1), 1)
     got = over_y(jnp.where(upper, low, high), 3)
     mine = jnp.where(upper, high, low) + got
     near, far, both = (swapped(mine, ("kpt",), lambda i, s=s: i ^ s) for s in (1, 2, 3))

time: 78 us -> 80.5 us (1.032)
  starting transfers between devices: 19.1 us -> 27.3 us
  waiting for transfers between devices: 30.5 us -> 25.4 us
    ppermute x14 -> x18, starting transfers between devices: 19.1 us -> 27.3 us  [swapped(): return lax.ppermute(x, axes, [(i, partner(i)) for i in range(count)])]
    ppermute x14 -> x18, waiting for transfers between devices: 30.5 us -> 25.4 us  [swapped(): return lax.ppermute(x, axes, [(i, partner(i)) for i in range(count)])]
  transfers between devices with their start and end apart: 14 -> 18, of which waited for: 13 -> 12; matrix products, arithmetic and copies ran while one was open for 1% -> 1% of each run, Pallas kernels for 2% -> 5%
where the time goes in v3:
time: 80.5 us; the launch traced here: 80 us
  starting transfers between devices  27.3 us (34%)
  waiting for transfers between devices  25.4 us (32%)
  Pallas kernels  22.6 us (28%)
  between operations  3.31 us (4%)
    ppermute x18, starting transfers between devices, swapped(): return lax.ppermute(x, axes, [(i, partner(i)) for i in range(count)])  27.3 us
    ppermute x18, waiting for transfers between devices, swapped(): return lax.ppermute(x, axes, [(i, partner(i)) for i in range(count)])  25.4 us
    pallas_call x1, Pallas kernels, forward(): pl.pallas_call(forward_kernel, out_shape=(jax.ShapeDtypeStruct(BLOCK, f32...  19 us
    pallas_call x1, Pallas kernels, third(): pl.pallas_call(third_kernel, out_shape=(jax.ShapeDtypeStruct((1, 2, N, N)...  1.82 us
    pallas_call x1, Pallas kernels, last(): pl.pallas_call(last_kernel, out_shape=(jax.ShapeDtypeStruct(HALF_BLOCK, f...  1.82 us
  transfers between devices with their start and end apart: 18, of which 12 were waited for; matrix products, arithmetic and copies ran while one was open for 1% of the time, Pallas kernels for 5%

profile of v3, /device:TPU:38, one launch (start us, length us, event | category | flops | bytes accessed | tf_op | source)
XLA Modules:
  0.0 80.0 jit_solution(16298827561889454875)
XLA Ops:
  3.2 19.0 %shard_map.131 = (f32[16,4,16,256]{3,2,1,0:T(8,128)S(1)}, f32[16,4,16,256]{3,2,1,0:T(8,128)S(1)}, bf16[13,2,256,256]{3,2,1,0:T(8,128)(2,1)S(1)}, f32[3,256,256]{2,1,0:T(8,128)S(1)}, f32[2,16,256]{2,1,0:T(8,128)S(1)}) custom-call(f32[1]{0:T(128)S(6)} %copy.14.refs_0_, f32[1]{0:T(128)S(6)} %copy.15.refs_1_, s32[1]{0:T(128)S(6)} %copy.16.refs_2_, ...), custom_call_target="tpu_custom_call" | custom-call | flops 13287555072 | bytes 8388608 | tf_op jit(solution)/shard_map/pallas_call | solution.py:361
  22.2 0.1 collective-permute-start
  22.3 1.8 %shard_map.132 = (bf16[1,2,256,256]{3,2,1,0:T(8,128)(2,1)S(1)}, f32[8,4,16,256]{3,2,1,0:T(8,128)S(1)}, f32[8,4,16,256]{3,2,1,0:T(8,128)S(1)}) custom-call(bf16[13,2,256,256]{3,2,1,0:T(8,128)(2,1)S(1)} %get-tuple-element.19.kept_pairs, f32[3,256,256]{2,1,0:T(8,128)S(1)} %get-tuple-element.20.kept_full), custom_call_target="tpu_custom_call" | custom-call | flops 1207959552 | bytes 8388608 | tf_op jit(solution)/shard_map/pallas_call | solution.py:393
  24.1 0.8 %collective-permute-done = f32[16,4,16,256]{3,2,1,0:T(8,128)S(1)} collective-permute-done((f32[16,4,16,256]{3,2,1,0:T(8,128)S(1)}, f32[16,4,16,256]{3,2,1,0:T(8,128)S(1)}, u32[]{:S(2)}, u32[]{:S(2)}) %collective-permute-start) | collective-permute-done | bytes 1048608 | tf_op jit(solution)/shard_map/ppermute | solution.py:433
  24.9 0.2 slice_add_fusion
  25.1 1.7 %collective-permute-start.1 = (f32[8,4,16,256]{3,2,1,0:T(8,128)S(1)}, f32[8,4,16,256]{3,2,1,0:T(8,128)S(1)}, u32[]{:S(2)}, u32[]{:S(2)}) collective-permute-start(f32[8,4,16,256]{3,2,1,0:T(8,128)S(1)} %get-tuple-element.24), channel_id=1, source_target_pairs={{0,1},{1,0},{2,3},{3,2},{16,48},{17,49},{18,50},{19,51},{32,33},{3... | collective-permute-start | bytes 1572872 | tf_op jit(solution)/shard_map/ppermute | solution.py:433
  26.8 0.0 collective-permute-start.5
  26.8 1.8 %shard_map.133 = (f32[8,4,16,256]{3,2,1,0:T(8,128)S(1)}, f32[8,4,16,256]{3,2,1,0:T(8,128)S(1)}) custom-call(bf16[13,2,256,256]{3,2,1,0:T(8,128)(2,1)S(1)} %get-tuple-element.19.kept_pairs, f32[3,256,256]{2,1,0:T(8,128)S(1)} %get-tuple-element.20.kept_full, bf16[1,2,256,256]{3,2,1,0:T(8,128)(2,1)S(1)} %get-tuple-element.27.next_pair), custom_call_target="tpu_custom_call" | custom-call | flops 1207959552 | bytes 8388608 | tf_op jit(solution)/shard_map/pallas_call | solution.py:414
  28.6 0.6 collective-permute-start.9
  29.3 5.2 %collective-permute-done.1 = f32[8,4,16,256]{3,2,1,0:T(8,128)S(1)} collective-permute-done((f32[8,4,16,256]{3,2,1,0:T(8,128)S(1)}, f32[8,4,16,256]{3,2,1,0:T(8,128)S(1)}, u32[]{:S(2)}, u32[]{:S(2)}) %collective-permute-start.1) | collective-permute-done | bytes 524320 | tf_op jit(solution)/shard_map/ppermute | solution.py:433
  34.4 0.1 slice_add_fusion.7
  34.5 0.2 collective-permute-start.2
  34.7 0.0 collective-permute-done.5
  34.7 0.1 slice_add_fusion.5
  34.8 0.9 %collective-permute-start.6 = (f32[4,4,16,256]{3,2,1,0:T(8,128)S(1)}, f32[4,4,16,256]{3,2,1,0:T(8,128)S(1)}, u32[]{:S(2)}, u32[]{:S(2)}) collective-permute-start(f32[4,4,16,256]{3,2,1,0:T(8,128)S(1)} %get-tuple-element.37), channel_id=1, source_target_pairs={{0,64},{16,208},{32,96},{48,240},{64,0},{80,144},{96,32},{112,176}... | collective-permute-start | bytes 786440 | tf_op jit(solution)/shard_map/ppermute | solution.py:433
  35.7 0.0 collective-permute-done.9
  35.7 0.1 slice_add_fusion.3
  35.8 1.3 %collective-permute-start.10 = (f32[4,4,16,256]{3,2,1,0:T(8,128)S(1)}, f32[4,4,16,256]{3,2,1,0:T(8,128)S(1)}, u32[]{:S(2)}, u32[]{:S(2)}) collective-permute-start(f32[4,4,16,256]{3,2,1,0:T(8,128)S(1)} %get-tuple-element.35), channel_id=1, source_target_pairs={{0,64},{16,208},{32,96},{48,240},{64,0},{80,144},{96,32},{112,176}... | collective-permute-start | bytes 786440 | tf_op jit(solution)/shard_map/ppermute | solution.py:433
  37.1 3.9 %collective-permute-done.2 = f32[4,4,16,256]{3,2,1,0:T(8,128)S(1)} collective-permute-done((f32[4,4,16,256]{3,2,1,0:T(8,128)S(1)}, f32[4,4,16,256]{3,2,1,0:T(8,128)S(1)}, u32[]{:S(2)}, u32[]{:S(2)}) %collective-permute-start.2) | collective-permute-done | bytes 262176 | tf_op jit(solution)/shard_map/ppermute | solution.py:433
  41.0 0.9 %collective-permute-start.3 = (f32[2,4,16,256]{3,2,1,0:T(8,128)S(1)}, f32[2,4,16,256]{3,2,1,0:T(8,128)S(1)}, u32[]{:S(2)}, u32[]{:S(2)}) collective-permute-start(f32[2,4,16,256]{3,2,1,0:T(8,128)S(1)} %get-tuple-element.45), channel_id=1, source_target_pairs={{0,64},{16,208},{32,96},{48,240},{64,0},{80,144},{96,32},{112,176}... | collective-permute-start | bytes 393224 | tf_op jit(solution)/shard_map/ppermute | solution.py:433
  41.9 0.0 collective-permute-done.6
  42.0 1.6 %collective-permute-start.7 = (f32[2,4,16,256]{3,2,1,0:T(8,128)S(1)}, f32[2,4,16,256]{3,2,1,0:T(8,128)S(1)}, u32[]{:S(2)}, u32[]{:S(2)}) collective-permute-start(f32[2,4,16,256]{3,2,1,0:T(8,128)S(1)} %get-tuple-element.43), channel_id=1, source_target_pairs={{0,192},{16,48},{32,224},{48,16},{64,128},{80,112},{96,160},{112,8... | collective-permute-start | bytes 393224 | tf_op jit(solution)/shard_map/ppermute | solution.py:433
  43.6 0.5 collective-permute-done.10
  44.1 2.5 %collective-permute-start.11 = (f32[2,4,16,256]{3,2,1,0:T(8,128)S(1)}, f32[2,4,16,256]{3,2,1,0:T(8,128)S(1)}, u32[]{:S(2)}, u32[]{:S(2)}) collective-permute-start(f32[2,4,16,256]{3,2,1,0:T(8,128)S(1)} %get-tuple-element.41), channel_id=1, source_target_pairs={{0,192},{16,48},{32,224},{48,16},{64,128},{80,112},{96,160},{112,8... | collective-permute-start | bytes 393224 | tf_op jit(solution)/shard_map/ppermute | solution.py:433
  46.6 1.6 %collective-permute-done.7 = f32[2,4,16,256]{3,2,1,0:T(8,128)S(1)} collective-permute-done((f32[2,4,16,256]{3,2,1,0:T(8,128)S(1)}, f32[2,4,16,256]{3,2,1,0:T(8,128)S(1)}, u32[]{:S(2)}, u32[]{:S(2)}) %collective-permute-start.7) | collective-permute-done | bytes 131104 | tf_op jit(solution)/shard_map/ppermute | solution.py:433
  48.2 1.3 %collective-permute-start.8 = (f32[1,4,16,256]{3,2,1,0:T(8,128)S(1)}, f32[1,4,16,256]{3,2,1,0:T(8,128)S(1)}, u32[]{:S(2)}, u32[]{:S(2)}) collective-permute-start(f32[1,4,16,256]{3,2,1,0:T(8,128)S(1)} %slice_add_fusion.16), channel_id=1, source_target_pairs={{0,32},{16,80},{32,0},{48,112},{64,96},{80,16},{96,64},{112,48},{1... | collective-permute-start | bytes 196616 | tf_op jit(solution)/shard_map/ppermute | solution.py:433
  49.6 1.0 %collective-permute-done.11 = f32[2,4,16,256]{3,2,1,0:T(8,128)S(1)} collective-permute-done((f32[2,4,16,256]{3,2,1,0:T(8,128)S(1)}, f32[2,4,16,256]{3,2,1,0:T(8,128)S(1)}, u32[]{:S(2)}, u32[]{:S(2)}) %collective-permute-start.11) | collective-permute-done | bytes 131104 | tf_op jit(solution)/shard_map/ppermute | solution.py:433
  50.6 2.0 %collective-permute-start.12 = (f32[1,4,16,256]{3,2,1,0:T(8,128)S(1)}, f32[1,4,16,256]{3,2,1,0:T(8,128)S(1)}, u32[]{:S(2)}, u32[]{:S(2)}) collective-permute-start(f32[1,4,16,256]{3,2,1,0:T(8,128)S(1)} %slice_add_fusion.14), channel_id=1, source_target_pairs={{0,32},{16,80},{32,0},{48,112},{64,96},{80,16},{96,64},{112,48},{1... | collective-permute-start | bytes 196616 | tf_op jit(solution)/shard_map/ppermute | solution.py:433
  52.6 0.0 collective-permute-done.3
  52.6 0.6 collective-permute-start.4
  53.3 0.0 collective-permute-done.8
  53.3 1.7 %collective-permute-done.12 = f32[1,4,16,256]{3,2,1,0:T(8,128)S(1)} collective-permute-done((f32[1,4,16,256]{3,2,1,0:T(8,128)S(1)}, f32[1,4,16,256]{3,2,1,0:T(8,128)S(1)}, u32[]{:S(2)}, u32[]{:S(2)}) %collective-permute-start.12) | collective-permute-done | bytes 65568 | tf_op jit(solution)/shard_map/ppermute | solution.py:433
  55.0 1.7 %collective-permute-start.13 = (f32[4,16,256]{2,1,0:T(8,128)S(1)}, f32[4,16,256]{2,1,0:T(8,128)S(1)}, u32[]{:S(2)}, u32[]{:S(2)}) collective-permute-start(f32[4,16,256]{2,1,0:T(8,128)S(1)} %broadcast_select_fusion), channel_id=1, source_target_pairs={{0,1},{1,0},{2,3},{3,2},{4,5},{5,4},{6,7},{7,6},{8,9},{9,8},{10,11... | collective-permute-start | bytes 196616 | tf_op jit(solution)/shard_map/ppermute | solution.py:433
  56.6 1.5 %collective-permute-done.4 = f32[1,4,16,256]{3,2,1,0:T(8,128)S(1)} collective-permute-done((f32[1,4,16,256]{3,2,1,0:T(8,128)S(1)}, f32[1,4,16,256]{3,2,1,0:T(8,128)S(1)}, u32[]{:S(2)}, u32[]{:S(2)}) %collective-permute-start.4) | collective-permute-done | bytes 65568 | tf_op jit(solution)/shard_map/ppermute | solution.py:433
  58.2 1.1 %collective-permute-done.13 = f32[4,16,256]{2,1,0:T(8,128)S(1)} collective-permute-done((f32[4,16,256]{2,1,0:T(8,128)S(1)}, f32[4,16,256]{2,1,0:T(8,128)S(1)}, u32[]{:S(2)}, u32[]{:S(2)}) %collective-permute-start.13) | collective-permute-done | bytes 65568 | tf_op jit(solution)/shard_map/ppermute | solution.py:433
  59.4 3.1 %collective-permute-start.14 = (f32[4,16,256]{2,1,0:T(8,128)S(1)}, f32[4,16,256]{2,1,0:T(8,128)S(1)}, u32[]{:S(2)}, u32[]{:S(2)}) collective-permute-start(f32[4,16,256]{2,1,0:T(8,128)S(1)} %get-tuple-element.30), channel_id=1, source_target_pairs={{0,3},{1,2},{2,1},{3,0},{4,7},{5,6},{6,5},{7,4},{8,11},{9,10},{10,... | collective-permute-start | bytes 196616 | tf_op jit(solution)/shard_map/ppermute | solution.py:433
  62.5 2.5 %collective-permute-done.14 = f32[4,16,256]{2,1,0:T(8,128)S(1)} collective-permute-done((f32[4,16,256]{2,1,0:T(8,128)S(1)}, f32[4,16,256]{2,1,0:T(8,128)S(1)}, u32[]{:S(2)}, u32[]{:S(2)}) %collective-permute-start.14) | collective-permute-done | bytes 65568 | tf_op jit(solution)/shard_map/ppermute | solution.py:433
  65.0 7.3 %collective-permute-start.16 = (f32[4,16,256]{2,1,0:T(8,128)S(1)}, f32[4,16,256]{2,1,0:T(8,128)S(1)}, u32[]{:S(2)}, u32[]{:S(2)}) collective-permute-start(f32[4,16,256]{2,1,0:T(8,128)S(1)} %select_add_fusion), channel_id=1, source_target_pairs={{0,8},{4,12},{8,0},{12,4},{1,9},{5,13},{9,1},{13,5},{2,10},{6,14},... | collective-permute-start | bytes 196616 | tf_op jit(solution)/shard_map/ppermute | solution.py:433
  72.3 0.0 collective-permute-start.17
  72.3 1.5 %collective-permute-start.15 = (f32[4,16,256]{2,1,0:T(8,128)S(1)}, f32[4,16,256]{2,1,0:T(8,128)S(1)}, u32[]{:S(2)}, u32[]{:S(2)}) collective-permute-start(f32[4,16,256]{2,1,0:T(8,128)S(1)} %select_add_fusion), channel_id=1, source_target_pairs={{0,4},{4,0},{8,12},{12,8},{1,5},{5,1},{9,13},{13,9},{2,6},{6,2},{1... | collective-permute-start | bytes 196616 | tf_op jit(solution)/shard_map/ppermute | solution.py:433
  73.7 1.2 %collective-permute-done.16 = f32[4,16,256]{2,1,0:T(8,128)S(1)} collective-permute-done((f32[4,16,256]{2,1,0:T(8,128)S(1)}, f32[4,16,256]{2,1,0:T(8,128)S(1)}, u32[]{:S(2)}, u32[]{:S(2)}) %collective-permute-start.16) | collective-permute-done | bytes 65568 | tf_op jit(solution)/shard_map/ppermute | solution.py:433
  74.9 4.4 %collective-permute-done.17 = f32[4,16,256]{2,1,0:T(8,128)S(1)} collective-permute-done((f32[4,16,256]{2,1,0:T(8,128)S(1)}, f32[4,16,256]{2,1,0:T(8,128)S(1)}, u32[]{:S(2)}, u32[]{:S(2)}) %collective-permute-start.17) | collective-permute-done | bytes 65568 | tf_op jit(solution)/shard_map/ppermute | solution.py:433
  79.3 0.0 collective-permute-done.15
  79.4 0.6 slice_bitcast_fusion
  (11 shorter events, 0.3 us)
Async XLA Ops:
  22.2 2.7 %collective-permute-start = (f32[16,4,16,256]{3,2,1,0:T(8,128)S(1)}, f32[16,4,16,256]{3,2,1,0:T(8,128)S(1)}, u32[]{:S(2)}, u32[]{:S(2)}) collective-permute-start(f32[16,4,16,256]{3,2,1,0:T(8,128)S(1)} %get-tuple-element.18), channel_id=1, source_target_pairs={{0,16},{16,0},{32,48},{48,32},{64,80},{80,64},{96,112},{112,96},{1... | collective-permute-start | bytes 3145736 | tf_op jit(solution)/shard_map/ppermute | solution.py:433
  25.1 9.3 %collective-permute-start.1 = (f32[8,4,16,256]{3,2,1,0:T(8,128)S(1)}, f32[8,4,16,256]{3,2,1,0:T(8,128)S(1)}, u32[]{:S(2)}, u32[]{:S(2)}) collective-permute-start(f32[8,4,16,256]{3,2,1,0:T(8,128)S(1)} %get-tuple-element.24), channel_id=1, source_target_pairs={{0,1},{1,0},{2,3},{3,2},{16,48},{17,49},{18,50},{19,51},{32,33},{3... | collective-permute-start | bytes 1572872 | tf_op jit(solution)/shard_map/ppermute | solution.py:433
  26.8 7.9 %collective-permute-start.5 = (f32[8,4,16,256]{3,2,1,0:T(8,128)S(1)}, f32[8,4,16,256]{3,2,1,0:T(8,128)S(1)}, u32[]{:S(2)}, u32[]{:S(2)}) collective-permute-start(f32[8,4,16,256]{3,2,1,0:T(8,128)S(1)} %get-tuple-element.26), channel_id=1, source_target_pairs={{0,16},{16,0},{32,48},{48,32},{64,80},{80,64},{96,112},{112,96},{1... | collective-permute-start | bytes 1572872 | tf_op jit(solution)/shard_map/ppermute | solution.py:433
  28.6 7.1 %collective-permute-start.9 = (f32[8,4,16,256]{3,2,1,0:T(8,128)S(1)}, f32[8,4,16,256]{3,2,1,0:T(8,128)S(1)}, u32[]{:S(2)}, u32[]{:S(2)}) collective-permute-start(f32[8,4,16,256]{3,2,1,0:T(8,128)S(1)} %get-tuple-element.29), channel_id=1, source_target_pairs={{0,16},{16,0},{32,48},{48,32},{64,80},{80,64},{96,112},{112,96},{1... | collective-permute-start | bytes 1572872 | tf_op jit(solution)/shard_map/ppermute | solution.py:433
  34.5 6.5 %collective-permute-start.2 = (f32[4,4,16,256]{3,2,1,0:T(8,128)S(1)}, f32[4,4,16,256]{3,2,1,0:T(8,128)S(1)}, u32[]{:S(2)}, u32[]{:S(2)}) collective-permute-start(f32[4,4,16,256]{3,2,1,0:T(8,128)S(1)} %get-tuple-element.39), channel_id=1, source_target_pairs={{0,32},{1,33},{2,34},{3,35},{16,17},{17,16},{18,19},{19,18},{32,0}... | collective-permute-start | bytes 786440 | tf_op jit(solution)/shard_map/ppermute | solution.py:433
  34.8 7.1 %collective-permute-start.6 = (f32[4,4,16,256]{3,2,1,0:T(8,128)S(1)}, f32[4,4,16,256]{3,2,1,0:T(8,128)S(1)}, u32[]{:S(2)}, u32[]{:S(2)}) collective-permute-start(f32[4,4,16,256]{3,2,1,0:T(8,128)S(1)} %get-tuple-element.37), channel_id=1, source_target_pairs={{0,64},{16,208},{32,96},{48,240},{64,0},{80,144},{96,32},{112,176}... | collective-permute-start | bytes 786440 | tf_op jit(solution)/shard_map/ppermute | solution.py:433
  35.8 8.3 %collective-permute-start.10 = (f32[4,4,16,256]{3,2,1,0:T(8,128)S(1)}, f32[4,4,16,256]{3,2,1,0:T(8,128)S(1)}, u32[]{:S(2)}, u32[]{:S(2)}) collective-permute-start(f32[4,4,16,256]{3,2,1,0:T(8,128)S(1)} %get-tuple-element.35), channel_id=1, source_target_pairs={{0,64},{16,208},{32,96},{48,240},{64,0},{80,144},{96,32},{112,176}... | collective-permute-start | bytes 786440 | tf_op jit(solution)/shard_map/ppermute | solution.py:433
  41.0 11.6 %collective-permute-start.3 = (f32[2,4,16,256]{3,2,1,0:T(8,128)S(1)}, f32[2,4,16,256]{3,2,1,0:T(8,128)S(1)}, u32[]{:S(2)}, u32[]{:S(2)}) collective-permute-start(f32[2,4,16,256]{3,2,1,0:T(8,128)S(1)} %get-tuple-element.45), channel_id=1, source_target_pairs={{0,64},{16,208},{32,96},{48,240},{64,0},{80,144},{96,32},{112,176}... | collective-permute-start | bytes 393224 | tf_op jit(solution)/shard_map/ppermute | solution.py:433
  42.0 6.3 %collective-permute-start.7 = (f32[2,4,16,256]{3,2,1,0:T(8,128)S(1)}, f32[2,4,16,256]{3,2,1,0:T(8,128)S(1)}, u32[]{:S(2)}, u32[]{:S(2)}) collective-permute-start(f32[2,4,16,256]{3,2,1,0:T(8,128)S(1)} %get-tuple-element.43), channel_id=1, source_target_pairs={{0,192},{16,48},{32,224},{48,16},{64,128},{80,112},{96,160},{112,8... | collective-permute-start | bytes 393224 | tf_op jit(solution)/shard_map/ppermute | solution.py:433
  44.1 6.5 %collective-permute-start.11 = (f32[2,4,16,256]{3,2,1,0:T(8,128)S(1)}, f32[2,4,16,256]{3,2,1,0:T(8,128)S(1)}, u32[]{:S(2)}, u32[]{:S(2)}) collective-permute-start(f32[2,4,16,256]{3,2,1,0:T(8,128)S(1)} %get-tuple-element.41), channel_id=1, source_target_pairs={{0,192},{16,48},{32,224},{48,16},{64,128},{80,112},{96,160},{112,8... | collective-permute-start | bytes 393224 | tf_op jit(solution)/shard_map/ppermute | solution.py:433
  48.2 5.0 %collective-permute-start.8 = (f32[1,4,16,256]{3,2,1,0:T(8,128)S(1)}, f32[1,4,16,256]{3,2,1,0:T(8,128)S(1)}, u32[]{:S(2)}, u32[]{:S(2)}) collective-permute-start(f32[1,4,16,256]{3,2,1,0:T(8,128)S(1)} %slice_add_fusion.16), channel_id=1, source_target_pairs={{0,32},{16,80},{32,0},{48,112},{64,96},{80,16},{96,64},{112,48},{1... | collective-permute-start | bytes 196616 | tf_op jit(solution)/shard_map/ppermute | solution.py:433
  50.6 4.4 %collective-permute-start.12 = (f32[1,4,16,256]{3,2,1,0:T(8,128)S(1)}, f32[1,4,16,256]{3,2,1,0:T(8,128)S(1)}, u32[]{:S(2)}, u32[]{:S(2)}) collective-permute-start(f32[1,4,16,256]{3,2,1,0:T(8,128)S(1)} %slice_add_fusion.14), channel_id=1, source_target_pairs={{0,32},{16,80},{32,0},{48,112},{64,96},{80,16},{96,64},{112,48},{1... | collective-permute-start | bytes 196616 | tf_op jit(solution)/shard_map/ppermute | solution.py:433
  52.6 5.6 %collective-permute-start.4 = (f32[1,4,16,256]{3,2,1,0:T(8,128)S(1)}, f32[1,4,16,256]{3,2,1,0:T(8,128)S(1)}, u32[]{:S(2)}, u32[]{:S(2)}) collective-permute-start(f32[1,4,16,256]{3,2,1,0:T(8,128)S(1)} %slice_add_fusion.18), channel_id=1, source_target_pairs={{0,192},{16,80},{32,224},{48,112},{64,128},{80,16},{96,160},{112,4... | collective-permute-start | bytes 196616 | tf_op jit(solution)/shard_map/ppermute | solution.py:433
  55.0 4.4 %collective-permute-start.13 = (f32[4,16,256]{2,1,0:T(8,128)S(1)}, f32[4,16,256]{2,1,0:T(8,128)S(1)}, u32[]{:S(2)}, u32[]{:S(2)}) collective-permute-start(f32[4,16,256]{2,1,0:T(8,128)S(1)} %broadcast_select_fusion), channel_id=1, source_target_pairs={{0,1},{1,0},{2,3},{3,2},{4,5},{5,4},{6,7},{7,6},{8,9},{9,8},{10,11... | collective-permute-start | bytes 196616 | tf_op jit(solution)/shard_map/ppermute | solution.py:433
  59.4 5.6 %collective-permute-start.14 = (f32[4,16,256]{2,1,0:T(8,128)S(1)}, f32[4,16,256]{2,1,0:T(8,128)S(1)}, u32[]{:S(2)}, u32[]{:S(2)}) collective-permute-start(f32[4,16,256]{2,1,0:T(8,128)S(1)} %get-tuple-element.30), channel_id=1, source_target_pairs={{0,3},{1,2},{2,1},{3,0},{4,7},{5,6},{6,5},{7,4},{8,11},{9,10},{10,... | collective-permute-start | bytes 196616 | tf_op jit(solution)/shard_map/ppermute | solution.py:433
  65.0 10.0 %collective-permute-start.16 = (f32[4,16,256]{2,1,0:T(8,128)S(1)}, f32[4,16,256]{2,1,0:T(8,128)S(1)}, u32[]{:S(2)}, u32[]{:S(2)}) collective-permute-start(f32[4,16,256]{2,1,0:T(8,128)S(1)} %select_add_fusion), channel_id=1, source_target_pairs={{0,8},{4,12},{8,0},{12,4},{1,9},{5,13},{9,1},{13,5},{2,10},{6,14},... | collective-permute-start | bytes 196616 | tf_op jit(solution)/shard_map/ppermute | solution.py:433
  72.3 7.1 %collective-permute-start.17 = (f32[4,16,256]{2,1,0:T(8,128)S(1)}, f32[4,16,256]{2,1,0:T(8,128)S(1)}, u32[]{:S(2)}, u32[]{:S(2)}) collective-permute-start(f32[4,16,256]{2,1,0:T(8,128)S(1)} %select_add_fusion), channel_id=1, source_target_pairs={{0,12},{4,8},{8,4},{12,0},{1,13},{5,9},{9,5},{13,1},{2,14},{6,10},... | collective-permute-start | bytes 196616 | tf_op jit(solution)/shard_map/ppermute | solution.py:433
  72.3 7.1 %collective-permute-start.15 = (f32[4,16,256]{2,1,0:T(8,128)S(1)}, f32[4,16,256]{2,1,0:T(8,128)S(1)}, u32[]{:S(2)}, u32[]{:S(2)}) collective-permute-start(f32[4,16,256]{2,1,0:T(8,128)S(1)} %select_add_fusion), channel_id=1, source_target_pairs={{0,4},{4,0},{8,12},{12,8},{1,5},{5,1},{9,13},{13,9},{2,6},{6,2},{1... | collective-permute-start | bytes 196616 | tf_op jit(solution)/shard_map/ppermute | solution.py:433

commit v4 on v3

--- a/solution.py
+++ b/solution.py
@@ -265,10 +265,14 @@
         gamma = source(i)
         pieces(lambda r, y: m.put(f"C{i % 2}", r, y + jnp.where(eye(r), gamma, 0.0)), m.mm(f"Vt{i - 1}", f"U{i - 1}"))
 
-    def dressed(i):
+    def dressed_re(i):
         s, d = names(i)
         C = f"C{i % 2}"
         pieces(lambda r, p: m.put(f"p{i % 2}", r, 0.5 * p), m.mm(d, C) + m.mm(s, C, True))
+
+    def dressed_im(i):
+        s, d = names(i)
+        C = f"C{i % 2}"
         pieces(lambda r, a, b: m.put(f"q{i % 2}", r, 0.5 * (a - b)), m.mm(s, C), m.mm(d, C, True))
 
     def lesser(i):
@@ -301,10 +305,12 @@
     for i in range(1, 5):
         own_energy(i)
         if i > 1:
-            dressed(i - 1)
+            dressed_re(i - 1)
         scale(i)
+        if i > 1:
+            dressed_im(i - 1)
+        square()
         lesser(i - 1)
-        square()
         lesser_turned(i - 1)
         green(i)
         lesser_hop(i - 1)
@@ -312,8 +318,9 @@
             hop(i)
         inflow(i)
     steps = {i: back_products(m, i, weight, done) for i in (3, 2, 1)}
-    dressed(4)
+    dressed_re(4)
     steps[3][3]()
+    dressed_im(4)
     lesser(4)
     steps[3][4]()
     steps[3][0]()
@@ -471,20 +478,30 @@
     keep_0, send_0 = last(kept_pairs, kept_full, next_pair)
     got_0 = over_core(send_0)
     low_1, low_0 = keep_1, keep_0
+    low_1, away_1 = halves(keep_1, got_1)
+    got_1 = over_x(away_1, 0)
+    low_0, away_0 = halves(keep_0, got_0)
+    got_0 = over_x(away_0, 0)
     for step in range(3):
-        low_1, away_1 = halves(low_1, got_1)
-        got_1 = over_mixed(away_1, step - 1) if step else over_x(away_1, 0)
-        low_0, away_0 = halves(low_0, got_0)
-        got_0 = over_mixed(away_0, step - 1) if step else over_x(away_0, 0)
         high, away_high = halves(high, got_high)
         got_high = over_x(away_high, step - 1) if step else over_rest(away_high, 1)
+        if step == 2:
+            break
+        if step:
+            low, away = halves(low, got)
+        else:
+            pairs = [halves(low_1, got_1), halves(low_0, got_0)]
+            low, away = (jnp.stack([p[n] for p in pairs], 1) for n in range(2))
+        got = over_mixed(away, step)
     high = high[0] + got_high[0]
-    low_1 = low_1[0] + got_1[0]
-    low_0 = low_0[0] + got_0[0]
+    low_1, low_0 = (low[0, n] + got[0, n] for n in range(2))
     odd, upper = sides[0] > 0.5, sides[1] > 0.5
-    low = jnp.where(odd, low_1, low_0) + over_y(jnp.where(odd, low_0, low_1), 1)
-    got = over_y(jnp.where(upper, low, high), 3)
-    mine = jnp.where(upper, high, low) + got
+    low, low_away = jnp.where(odd, low_1, low_0), jnp.where(odd, low_0, low_1)
+    count = lax.axis_size("layer") // 2
+    beside = lax.ppermute(low_away, "layer", [(i, i ^ 1) for i in range(count)])
+    across = lax.ppermute(low_away, "layer", [(i, i ^ 2) for i in range(count, 2 * count)])
+    opposite = over_y(jnp.where(upper, low, high), 3)
+    mine = (jnp.where(upper, high, low) + opposite) + (beside + across)
     near, far, both = (swapped(mine, ("kpt",), lambda i, s=s: i ^ s) for s in (1, 2, 3))
     total = (mine + near) + (far + both)
     return total[None, :2], total[None, 2:]

time: 80.5 us -> 83.5 us (1.037)
  waiting for transfers between devices: 25.4 us -> 27.4 us
  starting transfers between devices: 27.3 us -> 28.8 us
    ppermute x0 -> x2, starting transfers between devices: none -> 4.78 us  [the longest x1 3.49 us: per_device(): beside = lax.ppermute(low_away, 'layer', [(i, i ^ 1) for i in range(count)])]
    ppermute x18 -> x15, starting transfers between devices: 27.3 us -> 24 us  [swapped(): return lax.ppermute(x, axes, [(i, partner(i)) for i in range(count)])]
    ppermute x0 -> x2, waiting for transfers between devices: none -> 2.64 us  [the longest x1 2.64 us: per_device(): lax.ppermute(low_away, 'layer', [(i, i ^ 2) for i in range(count, 2 * cou...]
    ppermute x18 -> x15, waiting for transfers between devices: 25.4 us -> 24.8 us  [swapped(): return lax.ppermute(x, axes, [(i, partner(i)) for i in range(count)])]
  transfers between devices with their start and end apart: 18 -> 17, of which waited for: 12 -> 10; matrix products, arithmetic and copies ran while one was open for 1% -> 1% of each run, Pallas kernels for 5% -> 4%
where the time goes in v4:
time: 83.5 us; the launch traced here: 83 us
  starting transfers between devices  28.8 us (34%)
  waiting for transfers between devices  27.4 us (33%)
  Pallas kernels  22.1 us (26%)
  between operations  3.36 us (4%)
    ppermute x15, waiting for transfers between devices, swapped(): return lax.ppermute(x, axes, [(i, partner(i)) for i in range(count)])  24.8 us
    ppermute x15, starting transfers between devices, swapped(): return lax.ppermute(x, axes, [(i, partner(i)) for i in range(count)])  24 us
    pallas_call x1, Pallas kernels, forward(): pl.pallas_call(forward_kernel, out_shape=(jax.ShapeDtypeStruct(BLOCK, f32...  18.4 us
    ppermute x1, starting transfers between devices, per_device(): beside = lax.ppermute(low_away, 'layer', [(i, i ^ 1) for i in range(count)])  3.49 us
    ppermute x1, waiting for transfers between devices, per_device(): lax.ppermute(low_away, 'layer', [(i, i ^ 2) for i in range(count, 2 * cou...  2.64 us
    pallas_call x1, Pallas kernels, third(): pl.pallas_call(third_kernel, out_shape=(jax.ShapeDtypeStruct((1, 2, N, N)...  1.82 us
    pallas_call x1, Pallas kernels, last(): pl.pallas_call(last_kernel, out_shape=(jax.ShapeDtypeStruct(HALF_BLOCK, f...  1.82 us
  transfers between devices with their start and end apart: 17, of which 10 were waited for; matrix products, arithmetic and copies ran while one was open for 1% of the time, Pallas kernels for 4%

profile of v4, /device:TPU:38, one launch (start us, length us, event | category | flops | bytes accessed | tf_op | source)
XLA Modules:
  0.0 83.0 jit_solution(10894271244512926198)
XLA Ops:
  3.2 18.4 %shard_map.131 = (f32[16,4,16,256]{3,2,1,0:T(8,128)S(1)}, f32[16,4,16,256]{3,2,1,0:T(8,128)S(1)}, bf16[13,2,256,256]{3,2,1,0:T(8,128)(2,1)S(1)}, f32[3,256,256]{2,1,0:T(8,128)S(1)}, f32[2,16,256]{2,1,0:T(8,128)S(1)}) custom-call(f32[1]{0:T(128)S(6)} %copy.19.refs_0_, f32[1]{0:T(128)S(6)} %copy.20.refs_1_, s32[1]{0:T(128)S(6)} %copy.21.refs_2_, ...), custom_call_target="tpu_custom_call" | custom-call | flops 13287555072 | bytes 8388608 | tf_op jit(solution)/shard_map/pallas_call | solution.py:368
  21.7 0.1 collective-permute-start
  21.8 1.8 %shard_map.132 = (bf16[1,2,256,256]{3,2,1,0:T(8,128)(2,1)S(1)}, f32[8,4,16,256]{3,2,1,0:T(8,128)S(1)}, f32[8,4,16,256]{3,2,1,0:T(8,128)S(1)}) custom-call(bf16[13,2,256,256]{3,2,1,0:T(8,128)(2,1)S(1)} %get-tuple-element.19.kept_pairs, f32[3,256,256]{2,1,0:T(8,128)S(1)} %get-tuple-element.20.kept_full), custom_call_target="tpu_custom_call" | custom-call | flops 1207959552 | bytes 8388608 | tf_op jit(solution)/shard_map/pallas_call | solution.py:400
  23.6 0.8 collective-permute-done
  24.4 0.2 slice_add_fusion
  24.6 1.7 %collective-permute-start.1 = (f32[8,4,16,256]{3,2,1,0:T(8,128)S(1)}, f32[8,4,16,256]{3,2,1,0:T(8,128)S(1)}, u32[]{:S(2)}, u32[]{:S(2)}) collective-permute-start(f32[8,4,16,256]{3,2,1,0:T(8,128)S(1)} %get-tuple-element.24), channel_id=1, source_target_pairs={{0,1},{1,0},{2,3},{3,2},{16,48},{17,49},{18,50},{19,51},{32,33},{3... | collective-permute-start | bytes 1572872 | tf_op jit(solution)/shard_map/ppermute | solution.py:440
  26.3 1.8 %shard_map.133 = (f32[8,4,16,256]{3,2,1,0:T(8,128)S(1)}, f32[8,4,16,256]{3,2,1,0:T(8,128)S(1)}) custom-call(bf16[13,2,256,256]{3,2,1,0:T(8,128)(2,1)S(1)} %get-tuple-element.19.kept_pairs, f32[3,256,256]{2,1,0:T(8,128)S(1)} %get-tuple-element.20.kept_full, bf16[1,2,256,256]{3,2,1,0:T(8,128)(2,1)S(1)} %get-tuple-element.27.next_pair), custom_call_target="tpu_custom_call" | custom-call | flops 1207959552 | bytes 8388608 | tf_op jit(solution)/shard_map/pallas_call | solution.py:421
  28.1 0.1 collective-permute-start.7
  28.2 0.5 collective-permute-start.5
  28.7 5.2 %collective-permute-done.1 = f32[8,4,16,256]{3,2,1,0:T(8,128)S(1)} collective-permute-done((f32[8,4,16,256]{3,2,1,0:T(8,128)S(1)}, f32[8,4,16,256]{3,2,1,0:T(8,128)S(1)}, u32[]{:S(2)}, u32[]{:S(2)}) %collective-permute-start.1) | collective-permute-done | bytes 524320 | tf_op jit(solution)/shard_map/ppermute | solution.py:440
  33.9 0.1 slice_add_fusion.7
  34.0 0.2 collective-permute-start.2
  34.2 0.0 collective-permute-done.7
  34.2 0.1 slice_add_fusion.3
  34.3 0.9 %collective-permute-start.8 = (f32[4,4,16,256]{3,2,1,0:T(8,128)S(1)}, f32[4,4,16,256]{3,2,1,0:T(8,128)S(1)}, u32[]{:S(2)}, u32[]{:S(2)}) collective-permute-start(f32[4,4,16,256]{3,2,1,0:T(8,128)S(1)} %get-tuple-element.37), channel_id=1, source_target_pairs={{0,64},{16,208},{32,96},{48,240},{64,0},{80,144},{96,32},{112,176}... | collective-permute-start | bytes 786440 | tf_op jit(solution)/shard_map/ppermute | solution.py:440
  35.2 0.0 collective-permute-done.5
  35.2 0.1 slice_add_fusion.5
  35.3 1.3 %collective-permute-start.6 = (f32[4,4,16,256]{3,2,1,0:T(8,128)S(1)}, f32[4,4,16,256]{3,2,1,0:T(8,128)S(1)}, u32[]{:S(2)}, u32[]{:S(2)}) collective-permute-start(f32[4,4,16,256]{3,2,1,0:T(8,128)S(1)} %get-tuple-element.35), channel_id=1, source_target_pairs={{0,64},{16,208},{32,96},{48,240},{64,0},{80,144},{96,32},{112,176}... | collective-permute-start | bytes 786440 | tf_op jit(solution)/shard_map/ppermute | solution.py:440
  36.5 3.9 %collective-permute-done.2 = f32[4,4,16,256]{3,2,1,0:T(8,128)S(1)} collective-permute-done((f32[4,4,16,256]{3,2,1,0:T(8,128)S(1)}, f32[4,4,16,256]{3,2,1,0:T(8,128)S(1)}, u32[]{:S(2)}, u32[]{:S(2)}) %collective-permute-start.2) | collective-permute-done | bytes 262176 | tf_op jit(solution)/shard_map/ppermute | solution.py:440
  40.5 0.9 %collective-permute-start.3 = (f32[2,4,16,256]{3,2,1,0:T(8,128)S(1)}, f32[2,4,16,256]{3,2,1,0:T(8,128)S(1)}, u32[]{:S(2)}, u32[]{:S(2)}) collective-permute-start(f32[2,4,16,256]{3,2,1,0:T(8,128)S(1)} %get-tuple-element.39), channel_id=1, source_target_pairs={{0,64},{16,208},{32,96},{48,240},{64,0},{80,144},{96,32},{112,176}... | collective-permute-start | bytes 393224 | tf_op jit(solution)/shard_map/ppermute | solution.py:440
  41.4 0.0 collective-permute-done.8
  41.4 2.1 %collective-permute-done.6 = f32[4,4,16,256]{3,2,1,0:T(8,128)S(1)} collective-permute-done((f32[4,4,16,256]{3,2,1,0:T(8,128)S(1)}, f32[4,4,16,256]{3,2,1,0:T(8,128)S(1)}, u32[]{:S(2)}, u32[]{:S(2)}) %collective-permute-start.6) | collective-permute-done | bytes 262176 | tf_op jit(solution)/shard_map/ppermute | solution.py:440
  43.6 2.3 %collective-permute-start.9 = (f32[2,2,4,16,256]{4,3,2,0,1:T(8,128)S(1)}, f32[2,2,4,16,256]{4,3,2,0,1:T(8,128)S(1)}, u32[]{:S(2)}, u32[]{:S(2)}) collective-permute-start(f32[2,2,4,16,256]{4,3,2,0,1:T(8,128)S(1)} %pad_maximum_fusion), channel_id=1, source_target_pairs={{0,192},{16,48},{32,224},{48,16},{64,128},{80,112},{96,160},{112,8... | collective-permute-start | bytes 786440 | tf_op jit(solution)/shard_map/ppermute | solution.py:440
  45.9 0.0 collective-permute-done.3
  45.9 1.5 %collective-permute-start.4 = (f32[1,4,16,256]{3,2,1,0:T(8,128)S(1)}, f32[1,4,16,256]{3,2,1,0:T(8,128)S(1)}, u32[]{:S(2)}, u32[]{:S(2)}) collective-permute-start(f32[1,4,16,256]{3,2,1,0:T(8,128)S(1)} %slice_add_fusion.17), channel_id=1, source_target_pairs={{0,192},{16,80},{32,224},{48,112},{64,128},{80,16},{96,160},{112,4... | collective-permute-start | bytes 196616 | tf_op jit(solution)/shard_map/ppermute | solution.py:440
  47.4 3.8 %collective-permute-done.9 = f32[2,2,4,16,256]{4,3,2,0,1:T(8,128)S(1)} collective-permute-done((f32[2,2,4,16,256]{4,3,2,0,1:T(8,128)S(1)}, f32[2,2,4,16,256]{4,3,2,0,1:T(8,128)S(1)}, u32[]{:S(2)}, u32[]{:S(2)}) %collective-permute-start.9) | collective-permute-done | bytes 262176 | tf_op jit(solution)/shard_map/ppermute | solution.py:440
  51.3 2.0 %collective-permute-start.10 = (f32[1,2,4,16,256]{4,3,2,0,1:T(8,128)S(1)}, f32[1,2,4,16,256]{4,3,2,0,1:T(8,128)S(1)}, u32[]{:S(2)}, u32[]{:S(2)}) collective-permute-start(f32[1,2,4,16,256]{4,3,2,0,1:T(8,128)S(1)} %slice_add_fusion.8), channel_id=1, source_target_pairs={{0,32},{16,80},{32,0},{48,112},{64,96},{80,16},{96,64},{112,48},{1... | collective-permute-start | bytes 393224 | tf_op jit(solution)/shard_map/ppermute | solution.py:440
  53.3 0.0 collective-permute-done.4
  53.3 3.0 %collective-permute-done.10 = f32[1,2,4,16,256]{4,3,2,0,1:T(8,128)S(1)} collective-permute-done((f32[1,2,4,16,256]{4,3,2,0,1:T(8,128)S(1)}, f32[1,2,4,16,256]{4,3,2,0,1:T(8,128)S(1)}, u32[]{:S(2)}, u32[]{:S(2)}) %collective-permute-start.10) | collective-permute-done | bytes 131104 | tf_op jit(solution)/shard_map/ppermute | solution.py:440
  56.4 3.5 %collective-permute-start.12 = (f32[4,16,256]{2,1,0:T(8,128)S(1)}, f32[4,16,256]{2,1,0:T(8,128)S(1)}, u32[]{:S(2)}, u32[]{:S(2)}) collective-permute-start(f32[4,16,256]{2,1,0:T(8,128)S(1)} %get-tuple-element.45), channel_id=1, source_target_pairs={{0,1},{1,0},{4,5},{5,4},{8,9},{9,8},{12,13},{13,12},{16,17},{17,16... | collective-permute-start | bytes 196616 | tf_op jit(solution)/shard_map/ppermute | solution.py:501
  59.9 1.3 %collective-permute-start.13 = (f32[4,16,256]{2,1,0:T(8,128)S(1)}, f32[4,16,256]{2,1,0:T(8,128)S(1)}, u32[]{:S(2)}, u32[]{:S(2)}) collective-permute-start(f32[4,16,256]{2,1,0:T(8,128)S(1)} %get-tuple-element.45), channel_id=1, source_target_pairs={{2,0},{3,1},{6,4},{7,5},{10,8},{11,9},{14,12},{15,13},{18,16},{19,... | collective-permute-start | bytes 196616 | tf_op jit(solution)/shard_map/ppermute | solution.py:502
  61.2 3.8 %collective-permute-start.11 = (f32[4,16,256]{2,1,0:T(8,128)S(1)}, f32[4,16,256]{2,1,0:T(8,128)S(1)}, u32[]{:S(2)}, u32[]{:S(2)}) collective-permute-start(f32[4,16,256]{2,1,0:T(8,128)S(1)} %get-tuple-element.44), channel_id=1, source_target_pairs={{0,3},{1,2},{2,1},{3,0},{4,7},{5,6},{6,5},{7,4},{8,11},{9,10},{10,... | collective-permute-start | bytes 196616 | tf_op jit(solution)/shard_map/ppermute | solution.py:440
  65.0 0.0 collective-permute-done.12
  65.0 2.6 %collective-permute-done.13 = f32[4,16,256]{2,1,0:T(8,128)S(1)} collective-permute-done((f32[4,16,256]{2,1,0:T(8,128)S(1)}, f32[4,16,256]{2,1,0:T(8,128)S(1)}, u32[]{:S(2)}, u32[]{:S(2)}) %collective-permute-start.13) | collective-permute-done | bytes 65568 | tf_op jit(solution)/shard_map/ppermute | solution.py:502
  67.6 0.3 collective-permute-done.11
  67.9 0.1 add_add_fusion.1
  68.0 7.3 %collective-permute-start.15 = (f32[4,16,256]{2,1,0:T(8,128)S(1)}, f32[4,16,256]{2,1,0:T(8,128)S(1)}, u32[]{:S(2)}, u32[]{:S(2)}) collective-permute-start(f32[4,16,256]{2,1,0:T(8,128)S(1)} %add_add_fusion.1), channel_id=1, source_target_pairs={{0,8},{4,12},{8,0},{12,4},{1,9},{5,13},{9,1},{13,5},{2,10},{6,14},... | collective-permute-start | bytes 196616 | tf_op jit(solution)/shard_map/ppermute | solution.py:440
  75.3 0.0 collective-permute-start.16
  75.3 1.5 %collective-permute-start.14 = (f32[4,16,256]{2,1,0:T(8,128)S(1)}, f32[4,16,256]{2,1,0:T(8,128)S(1)}, u32[]{:S(2)}, u32[]{:S(2)}) collective-permute-start(f32[4,16,256]{2,1,0:T(8,128)S(1)} %add_add_fusion.1), channel_id=1, source_target_pairs={{0,4},{4,0},{8,12},{12,8},{1,5},{5,1},{9,13},{13,9},{2,6},{6,2},{1... | collective-permute-start | bytes 196616 | tf_op jit(solution)/shard_map/ppermute | solution.py:440
  76.7 1.1 %collective-permute-done.15 = f32[4,16,256]{2,1,0:T(8,128)S(1)} collective-permute-done((f32[4,16,256]{2,1,0:T(8,128)S(1)}, f32[4,16,256]{2,1,0:T(8,128)S(1)}, u32[]{:S(2)}, u32[]{:S(2)}) %collective-permute-start.15) | collective-permute-done | bytes 65568 | tf_op jit(solution)/shard_map/ppermute | solution.py:440
  77.8 4.5 %collective-permute-done.16 = f32[4,16,256]{2,1,0:T(8,128)S(1)} collective-permute-done((f32[4,16,256]{2,1,0:T(8,128)S(1)}, f32[4,16,256]{2,1,0:T(8,128)S(1)}, u32[]{:S(2)}, u32[]{:S(2)}) %collective-permute-start.16) | collective-permute-done | bytes 65568 | tf_op jit(solution)/shard_map/ppermute | solution.py:440
  82.4 0.0 collective-permute-done.14
  82.4 0.6 slice_bitcast_fusion.2
  (10 shorter events, 0.3 us)
Async XLA Ops:
  21.7 2.7 %collective-permute-start = (f32[16,4,16,256]{3,2,1,0:T(8,128)S(1)}, f32[16,4,16,256]{3,2,1,0:T(8,128)S(1)}, u32[]{:S(2)}, u32[]{:S(2)}) collective-permute-start(f32[16,4,16,256]{3,2,1,0:T(8,128)S(1)} %get-tuple-element.18), channel_id=1, source_target_pairs={{0,16},{16,0},{32,48},{48,32},{64,80},{80,64},{96,112},{112,96},{1... | collective-permute-start | bytes 3145736 | tf_op jit(solution)/shard_map/ppermute | solution.py:440
  24.6 9.3 %collective-permute-start.1 = (f32[8,4,16,256]{3,2,1,0:T(8,128)S(1)}, f32[8,4,16,256]{3,2,1,0:T(8,128)S(1)}, u32[]{:S(2)}, u32[]{:S(2)}) collective-permute-start(f32[8,4,16,256]{3,2,1,0:T(8,128)S(1)} %get-tuple-element.24), channel_id=1, source_target_pairs={{0,1},{1,0},{2,3},{3,2},{16,48},{17,49},{18,50},{19,51},{32,33},{3... | collective-permute-start | bytes 1572872 | tf_op jit(solution)/shard_map/ppermute | solution.py:440
  28.1 6.1 %collective-permute-start.7 = (f32[8,4,16,256]{3,2,1,0:T(8,128)S(1)}, f32[8,4,16,256]{3,2,1,0:T(8,128)S(1)}, u32[]{:S(2)}, u32[]{:S(2)}) collective-permute-start(f32[8,4,16,256]{3,2,1,0:T(8,128)S(1)} %get-tuple-element.29), channel_id=1, source_target_pairs={{0,16},{16,0},{32,48},{48,32},{64,80},{80,64},{96,112},{112,96},{1... | collective-permute-start | bytes 1572872 | tf_op jit(solution)/shard_map/ppermute | solution.py:440
  28.2 7.0 %collective-permute-start.5 = (f32[8,4,16,256]{3,2,1,0:T(8,128)S(1)}, f32[8,4,16,256]{3,2,1,0:T(8,128)S(1)}, u32[]{:S(2)}, u32[]{:S(2)}) collective-permute-start(f32[8,4,16,256]{3,2,1,0:T(8,128)S(1)} %get-tuple-element.26), channel_id=1, source_target_pairs={{0,16},{16,0},{32,48},{48,32},{64,80},{80,64},{96,112},{112,96},{1... | collective-permute-start | bytes 1572872 | tf_op jit(solution)/shard_map/ppermute | solution.py:440
  34.0 6.5 %collective-permute-start.2 = (f32[4,4,16,256]{3,2,1,0:T(8,128)S(1)}, f32[4,4,16,256]{3,2,1,0:T(8,128)S(1)}, u32[]{:S(2)}, u32[]{:S(2)}) collective-permute-start(f32[4,4,16,256]{3,2,1,0:T(8,128)S(1)} %get-tuple-element.33), channel_id=1, source_target_pairs={{0,32},{1,33},{2,34},{3,35},{16,17},{17,16},{18,19},{19,18},{32,0}... | collective-permute-start | bytes 786440 | tf_op jit(solution)/shard_map/ppermute | solution.py:440
  34.3 7.1 %collective-permute-start.8 = (f32[4,4,16,256]{3,2,1,0:T(8,128)S(1)}, f32[4,4,16,256]{3,2,1,0:T(8,128)S(1)}, u32[]{:S(2)}, u32[]{:S(2)}) collective-permute-start(f32[4,4,16,256]{3,2,1,0:T(8,128)S(1)} %get-tuple-element.37), channel_id=1, source_target_pairs={{0,64},{16,208},{32,96},{48,240},{64,0},{80,144},{96,32},{112,176}... | collective-permute-start | bytes 786440 | tf_op jit(solution)/shard_map/ppermute | solution.py:440
  35.3 8.3 %collective-permute-start.6 = (f32[4,4,16,256]{3,2,1,0:T(8,128)S(1)}, f32[4,4,16,256]{3,2,1,0:T(8,128)S(1)}, u32[]{:S(2)}, u32[]{:S(2)}) collective-permute-start(f32[4,4,16,256]{3,2,1,0:T(8,128)S(1)} %get-tuple-element.35), channel_id=1, source_target_pairs={{0,64},{16,208},{32,96},{48,240},{64,0},{80,144},{96,32},{112,176}... | collective-permute-start | bytes 786440 | tf_op jit(solution)/shard_map/ppermute | solution.py:440
  40.5 5.4 %collective-permute-start.3 = (f32[2,4,16,256]{3,2,1,0:T(8,128)S(1)}, f32[2,4,16,256]{3,2,1,0:T(8,128)S(1)}, u32[]{:S(2)}, u32[]{:S(2)}) collective-permute-start(f32[2,4,16,256]{3,2,1,0:T(8,128)S(1)} %get-tuple-element.39), channel_id=1, source_target_pairs={{0,64},{16,208},{32,96},{48,240},{64,0},{80,144},{96,32},{112,176}... | collective-permute-start | bytes 393224 | tf_op jit(solution)/shard_map/ppermute | solution.py:440
  43.6 7.7 %collective-permute-start.9 = (f32[2,2,4,16,256]{4,3,2,0,1:T(8,128)S(1)}, f32[2,2,4,16,256]{4,3,2,0,1:T(8,128)S(1)}, u32[]{:S(2)}, u32[]{:S(2)}) collective-permute-start(f32[2,2,4,16,256]{4,3,2,0,1:T(8,128)S(1)} %pad_maximum_fusion), channel_id=1, source_target_pairs={{0,192},{16,48},{32,224},{48,16},{64,128},{80,112},{96,160},{112,8... | collective-permute-start | bytes 786440 | tf_op jit(solution)/shard_map/ppermute | solution.py:440
  45.9 7.4 %collective-permute-start.4 = (f32[1,4,16,256]{3,2,1,0:T(8,128)S(1)}, f32[1,4,16,256]{3,2,1,0:T(8,128)S(1)}, u32[]{:S(2)}, u32[]{:S(2)}) collective-permute-start(f32[1,4,16,256]{3,2,1,0:T(8,128)S(1)} %slice_add_fusion.17), channel_id=1, source_target_pairs={{0,192},{16,80},{32,224},{48,112},{64,128},{80,16},{96,160},{112,4... | collective-permute-start | bytes 196616 | tf_op jit(solution)/shard_map/ppermute | solution.py:440
  51.3 5.1 %collective-permute-start.10 = (f32[1,2,4,16,256]{4,3,2,0,1:T(8,128)S(1)}, f32[1,2,4,16,256]{4,3,2,0,1:T(8,128)S(1)}, u32[]{:S(2)}, u32[]{:S(2)}) collective-permute-start(f32[1,2,4,16,256]{4,3,2,0,1:T(8,128)S(1)} %slice_add_fusion.8), channel_id=1, source_target_pairs={{0,32},{16,80},{32,0},{48,112},{64,96},{80,16},{96,64},{112,48},{1... | collective-permute-start | bytes 393224 | tf_op jit(solution)/shard_map/ppermute | solution.py:440
  56.4 8.6 %collective-permute-start.12 = (f32[4,16,256]{2,1,0:T(8,128)S(1)}, f32[4,16,256]{2,1,0:T(8,128)S(1)}, u32[]{:S(2)}, u32[]{:S(2)}) collective-permute-start(f32[4,16,256]{2,1,0:T(8,128)S(1)} %get-tuple-element.45), channel_id=1, source_target_pairs={{0,1},{1,0},{4,5},{5,4},{8,9},{9,8},{12,13},{13,12},{16,17},{17,16... | collective-permute-start | bytes 196616 | tf_op jit(solution)/shard_map/ppermute | solution.py:501
  59.9 7.8 %collective-permute-start.13 = (f32[4,16,256]{2,1,0:T(8,128)S(1)}, f32[4,16,256]{2,1,0:T(8,128)S(1)}, u32[]{:S(2)}, u32[]{:S(2)}) collective-permute-start(f32[4,16,256]{2,1,0:T(8,128)S(1)} %get-tuple-element.45), channel_id=1, source_target_pairs={{2,0},{3,1},{6,4},{7,5},{10,8},{11,9},{14,12},{15,13},{18,16},{19,... | collective-permute-start | bytes 196616 | tf_op jit(solution)/shard_map/ppermute | solution.py:502
  61.2 6.8 %collective-permute-start.11 = (f32[4,16,256]{2,1,0:T(8,128)S(1)}, f32[4,16,256]{2,1,0:T(8,128)S(1)}, u32[]{:S(2)}, u32[]{:S(2)}) collective-permute-start(f32[4,16,256]{2,1,0:T(8,128)S(1)} %get-tuple-element.44), channel_id=1, source_target_pairs={{0,3},{1,2},{2,1},{3,0},{4,7},{5,6},{6,5},{7,4},{8,11},{9,10},{10,... | collective-permute-start | bytes 196616 | tf_op jit(solution)/shard_map/ppermute | solution.py:440
  68.0 9.8 %collective-permute-start.15 = (f32[4,16,256]{2,1,0:T(8,128)S(1)}, f32[4,16,256]{2,1,0:T(8,128)S(1)}, u32[]{:S(2)}, u32[]{:S(2)}) collective-permute-start(f32[4,16,256]{2,1,0:T(8,128)S(1)} %add_add_fusion.1), channel_id=1, source_target_pairs={{0,8},{4,12},{8,0},{12,4},{1,9},{5,13},{9,1},{13,5},{2,10},{6,14},... | collective-permute-start | bytes 196616 | tf_op jit(solution)/shard_map/ppermute | solution.py:440
  75.3 7.1 %collective-permute-start.16 = (f32[4,16,256]{2,1,0:T(8,128)S(1)}, f32[4,16,256]{2,1,0:T(8,128)S(1)}, u32[]{:S(2)}, u32[]{:S(2)}) collective-permute-start(f32[4,16,256]{2,1,0:T(8,128)S(1)} %add_add_fusion.1), channel_id=1, source_target_pairs={{0,12},{4,8},{8,4},{12,0},{1,13},{5,9},{9,5},{13,1},{2,14},{6,10},... | collective-permute-start | bytes 196616 | tf_op jit(solution)/shard_map/ppermute | solution.py:440
  75.3 7.1 %collective-permute-start.14 = (f32[4,16,256]{2,1,0:T(8,128)S(1)}, f32[4,16,256]{2,1,0:T(8,128)S(1)}, u32[]{:S(2)}, u32[]{:S(2)}) collective-permute-start(f32[4,16,256]{2,1,0:T(8,128)S(1)} %add_add_fusion.1), channel_id=1, source_target_pairs={{0,4},{4,0},{8,12},{12,8},{1,5},{5,1},{9,13},{13,9},{2,6},{6,2},{1... | collective-permute-start | bytes 196616 | tf_op jit(solution)/shard_map/ppermute | solution.py:440
